TPU v7x, 256 devices: a 4x2x16 block of a 4x16x16 slice. The times are simulated.
256 devices in a mesh: parts: 2 (over y), seq: 16 (over z), head: 4 (over x), rep: 2 (over core).
Axes of the slice: x: 4, y: 2, z: 16, core: 2. Of those that a mesh axis runs over, the one named last changes fastest.
The devices are a block of a 4x16x16 slice.
Arguments:
- queries: bfloat16 [4, 4096, 2048], P(('parts', 'rep'), 'seq', 'head'), parts along dimension 0, may hold values from -6 to 6
- reflect_keys: bfloat16 [4, 4096, 2, 2048], P(('parts', 'rep'), 'seq', None, 'head'), parts along dimension 0, may hold values from -6 to 6
- reflect_values: bfloat16 [4, 4096, 2, 2048], P(('parts', 'rep'), 'seq', None, 'head'), parts along dimension 0, may hold values from -6 to 6
- reflect_beta: float32 [4, 4096, 2, 16], P(('parts', 'rep'), 'seq', None, 'head'), parts along dimension 0, may hold values from 0.2 to 2
- log_decay: float32 [4, 4096, 16], P(('parts', 'rep'), 'seq', 'head'), parts along dimension 0, may hold values from -2.5 to 0
- prompt_lengths: int32 [4, 6], P(('parts', 'rep')), parts along dimension 0, may hold values from 1 to 2048, 4096 in all within a row
- norm_gain: float32 [128], replicated, may hold values from 0.1 to 1.9
- out_weight: bfloat16 [2048, 2048], P('head'), may hold values from -0.125 to 0.125
Outputs:
- layer_out: bfloat16 [4, 4096, 2048], P(('parts', 'rep'), ('seq', 'head')), parts along dimension 0
There are 2 independent parts, one for each index of `parts`. A program takes and returns all parts, laid end to end along the dimension named above; an argument that names none is the same for every part. Nothing has to cross between parts.
Inputs may be any that keep to these rules, and one draw needn't show every extreme that they name: `prompt_lengths`: the 6 prompts of a pack lie end to end from its first token and cover all 4096 tokens; the longest has exactly 2048.
All inputs are finite; a program needn't handle non-finite values.
Results may differ from a plain program's by a relative error of at most 0.0095.
Values may be sent and summed in bfloat16 or wider, within the bound.
A program may use at most 64 MiB of HBM per device.

v0:
```python
import jax
import jax.numpy as jnp
from jax import lax
from jax.sharding import PartitionSpec as P

BLOCK = 64


highest = lax.Precision.HIGHEST
epsilon = 1e-06


def shifted(value, axis, steps):
    count = lax.axis_size(axis)
    initial, last = (max(0, -steps), min(count, count - steps))
    return lax.ppermute(value, axis, [(source, source + steps) for source in range(initial, last)])


def cut_along(array, dim, length):
    lengths = array.shape
    parts = array.reshape(*lengths[:dim], length, lengths[dim] // length, *lengths[dim + 1 :])
    return jnp.moveaxis(parts, dim, 0)


def summed_on_arrival(array, axis, dim):
    parts = cut_along(array, dim, lax.axis_size(axis))
    arrived = lax.all_to_all(parts, axis, split_axis=0, concat_axis=0, tiled=True)
    return arrived.astype(jnp.float32).sum(axis=0)


def unit_rows(vectors):
    return vectors * lax.rsqrt(jnp.sum(vectors * vectors, axis=-1, keepdims=True) + epsilon)


def block_parts(key_rows, value_rows, beta_rows, decay_rows, seg_rows, seg_before):
    steps_here = key_rows.shape[-2]
    cum_decay = jnp.cumsum(decay_rows, axis=-1)
    ordinal = jnp.arange(steps_here)
    incl_mask = ordinal[:, None] >= ordinal[None, :]
    strict_mask = ordinal[:, None] > ordinal[None, :]
    same_doc = seg_rows[:, None, :, None] == seg_rows[:, None, None, :]
    decay_gap = cum_decay[..., :, None] - cum_decay[..., None, :]
    decay_ratio = jnp.where(incl_mask & same_doc, jnp.exp(jnp.minimum(decay_gap, 0.0)), 0.0)
    carry_in = jnp.where(seg_rows[:, None, :] == seg_before[:, None, None], jnp.exp(cum_decay), 0.0)
    key_inner = jnp.einsum("bhik,bhjk->bhij", key_rows, key_rows, precision=highest)
    system = jnp.eye(steps_here, dtype=key_rows.dtype) + jnp.where(
        strict_mask, beta_rows[..., :, None] * decay_ratio * key_inner, 0.0
    )
    right_side = jnp.concatenate(
        [beta_rows[..., None] * value_rows, (beta_rows * carry_in)[..., None] * key_rows], axis=-1
    )
    solved = lax.linalg.triangular_solve(
        system, right_side, left_side=True, lower=True, unit_diagonal=True
    )
    val_width = value_rows.shape[-1]
    return (decay_ratio, carry_in, solved[..., :val_width], solved[..., val_width:])


def heads_product(left_maps, right_maps):
    return jnp.einsum("hij,hjk->hik", left_maps, right_maps, precision=highest)


def body(
    queries,
    reflect_keys,
    reflect_values,
    reflect_beta,
    log_decay,
    prompt_lengths,
    norm_gain,
    out_weight,
):
    tokens_here = queries.shape[1]
    refl_count = reflect_keys.shape[2]
    heads_here = reflect_beta.shape[3]
    head_width = queries.shape[2] // heads_here
    blocks = tokens_here // BLOCK
    sub_steps = refl_count * BLOCK
    offset = lax.axis_index("seq") * tokens_here
    doc_ends = jnp.cumsum(prompt_lengths[0])
    positions = offset + jnp.arange(tokens_here, dtype=jnp.int32)
    segment = jnp.sum((positions[:, None] >= doc_ends[None, :]).astype(jnp.int32), axis=-1)
    block_starts = positions[::BLOCK] - 1
    earlier_seg = jnp.sum((block_starts[:, None] >= doc_ends[None, :]).astype(jnp.int32), axis=-1)
    seg_before = jnp.where(block_starts < 0, -1, earlier_seg)
    seg_rows = jnp.repeat(segment.reshape(blocks, BLOCK), refl_count, axis=-1)
    query_rows = unit_rows(
        queries[0].astype(jnp.float32).reshape(blocks, BLOCK, heads_here, head_width)
    ) * head_width ** (-0.5)
    query_rows = query_rows.transpose(0, 2, 1, 3)
    key_rows = unit_rows(
        reflect_keys[0]
        .astype(jnp.float32)
        .reshape(blocks, BLOCK, refl_count, heads_here, head_width)
    )
    key_rows = key_rows.transpose(0, 3, 1, 2, 4).reshape(blocks, heads_here, sub_steps, head_width)
    value_rows = (
        reflect_values[0]
        .astype(jnp.float32)
        .reshape(blocks, BLOCK, refl_count, heads_here, head_width)
    )
    value_rows = value_rows.transpose(0, 3, 1, 2, 4).reshape(
        blocks, heads_here, sub_steps, head_width
    )
    beta_rows = (
        reflect_beta[0]
        .reshape(blocks, BLOCK, refl_count, heads_here)
        .transpose(0, 3, 1, 2)
        .reshape(blocks, heads_here, sub_steps)
    )
    gate_rows = log_decay[0].reshape(blocks, BLOCK, heads_here).transpose(0, 2, 1)
    decay_rows = jnp.concatenate(
        [gate_rows[..., None], jnp.zeros(gate_rows.shape + (refl_count - 1,), jnp.float32)], axis=-1
    ).reshape(blocks, heads_here, sub_steps)
    decay_ratio, carry_in, write_vals, write_keys = block_parts(
        key_rows, value_rows, beta_rows, decay_rows, seg_rows, seg_before
    )
    last_row = refl_count - 1
    read_weights = decay_ratio[..., last_row::refl_count, :] * jnp.einsum(
        "bhik,bhjk->bhij", query_rows, key_rows, precision=highest
    )
    carry_read = carry_in[..., last_row::refl_count]
    end_keys = decay_ratio[..., -1, :, None] * key_rows
    block_maps = carry_in[..., -1, None, None] * jnp.eye(
        head_width, dtype=jnp.float32
    ) - jnp.einsum("bhjk,bhjl->bhkl", end_keys, write_keys, precision=highest)
    block_adds = jnp.einsum("bhjk,bhjl->bhkl", end_keys, write_vals, precision=highest)
    identity_maps = jnp.broadcast_to(
        jnp.eye(head_width, dtype=jnp.float32), (heads_here, head_width, head_width)
    )
    zero_states = jnp.zeros((heads_here, head_width, head_width), jnp.float32)

    def compose_only(totals, step_pair):
        joined = (
            heads_product(step_pair[0], totals[0]),
            heads_product(step_pair[0], totals[1]) + step_pair[1],
        )
        return (joined, None)

    (device_map, device_add), unused = lax.scan(
        compose_only, (identity_maps, zero_states), (block_maps, block_adds)
    )

    def advance_hop(turn_index, current):
        return shifted(
            (heads_product(device_map, current) + device_add).astype(jnp.bfloat16), "seq", 1
        ).astype(jnp.float32)

    incoming = lax.fori_loop(0, lax.axis_size("seq") - 1, advance_hop, zero_states)

    def advance_block(current, step_pair):
        return (heads_product(step_pair[0], current) + step_pair[1], current)

    finished, block_start = lax.scan(advance_block, incoming, (block_maps, block_adds))
    updates = write_vals - jnp.einsum("bhck,bhkv->bhcv", write_keys, block_start, precision=highest)
    head_out = carry_read[..., None] * jnp.einsum(
        "bhik,bhkv->bhiv", query_rows, block_start, precision=highest
    ) + jnp.einsum("bhij,bhjv->bhiv", read_weights, updates, precision=highest)
    normed = (
        head_out
        * lax.rsqrt(jnp.mean(head_out * head_out, axis=-1, keepdims=True) + epsilon)
        * norm_gain
    ).astype(jnp.bfloat16)
    flat_rows = normed.transpose(0, 2, 1, 3).reshape(tokens_here, heads_here * head_width)
    layer_out = summed_on_arrival(
        jnp.dot(flat_rows, out_weight, preferred_element_type=jnp.float32).astype(jnp.bfloat16),
        "head",
        0,
    )
    return layer_out.astype(jnp.bfloat16)[None]


def solution(mesh):
    in_specs = (
        P(("parts", "rep"), "seq", "head"),
        P(("parts", "rep"), "seq", None, "head"),
        P(("parts", "rep"), "seq", None, "head"),
        P(("parts", "rep"), "seq", None, "head"),
        P(("parts", "rep"), "seq", "head"),
        P(("parts", "rep"), None),
        P(),
        P("head", None),
    )
    out_specs = P(("parts", "rep"), ("seq", "head"), None)
    return jax.shard_map(body, mesh=mesh, in_specs=in_specs, out_specs=out_specs, check_vma=False)
```

profile of v0, /device:TPU:1056, one launch (start us, length us, event | category | flops | bytes accessed | tf_op | source)
XLA Modules:
  0.0 373.8 jit_solution(6007310271413440816)
XLA Ops:
  9.2 3.2 slice.31
  21.8 3.4 fusion.27
  25.2 158.7 %custom-call.3 = f32[4,4,1,128,128]{3,4,2,1,0:T(8,128)} custom-call(f32[4,4,1,128,128]{4,3,2,1,0:T(8,128)} %fusion.27), custom_call_target="InvertDiagBlocksLowerTriangular" | custom-call | tf_op jit(solution)/shard_map/triangular_solve | solution.py:52
  193.7 3.3 convolution_subtract_fusion.1
  196.9 11.4 %while.40 = (s32[]{:T(128)}, f32[4,128,128]{2,1,0:T(8,128)S(1)}, f32[4,128,128]{2,1,0:T(8,128)S(1)}, f32[4,4,128,128]{3,2,1,0:T(8,128)}, f32[4,4,128,128]{3,2,1,0:T(8,128)}) while((s32[]{:T(128)}, f32[4,128,128]{2,1,0:T(8,128)S(1)}, f32[4,128,128]{2,1,0:T(8,128)S(1)}, f32[4,4,128,128]{3,2,1,0:T(8,128)}, ...), condition=%wide.region_7.8_spmd.clone.clone, body=%wide.region_6.7_spmd.clone.sunk.clone | while | flops 201457664 | bytes 2885202 | solution.py:140
  208.4 131.0 %while.41 = (s32[]{:T(128)}, f32[4,128,128]{2,1,0:T(8,128)S(1)}, f32[4,128,128]{2,1,0:T(8,128)S(1)}, f32[4,128,128]{2,1,0:T(8,128)S(1)}) while((s32[]{:T(128)}, f32[4,128,128]{2,1,0:T(8,128)S(1)}, f32[4,128,128]{2,1,0:T(8,128)S(1)}, f32[4,128,128]{2,1,0:T(8,128)S(1)}) %tuple.69), condition=%wide.region_9.10_spmd.clone.clone, body=%wide.region_8.9_spmd.clone.sunk.clone | while | flops 100925440 | bytes 1835111 | solution.py:149
  208.8 3.8 %collective-permute-start = (bf16[4,128,128]{2,1,0:T(8,128)(2,1)S(1)}, bf16[4,128,128]{2,1,0:T(8,128)(2,1)S(1)}, u32[]{:S(2)}, u32[]{:S(2)}) collective-permute-start(bf16[4,128,128]{2,1,0:T(8,128)(2,1)S(1)} %fusion.89), channel_id=1, source_target_pairs={{0,8},{8,16},{16,24},{24,32},{32,40},{40,48},{48,56},{56,64},{64,7... | collective-permute-start | bytes 393224 | tf_op jit(solution)/shard_map/while/body/eval_jaxpr/ppermute | solution.py:16
  212.6 4.6 %collective-permute-done = bf16[4,128,128]{2,1,0:T(8,128)(2,1)S(1)} collective-permute-done((bf16[4,128,128]{2,1,0:T(8,128)(2,1)S(1)}, bf16[4,128,128]{2,1,0:T(8,128)(2,1)S(1)}, u32[]{:S(2)}, u32[]{:S(2)}) %collective-permute-start) | collective-permute-done | bytes 131104 | tf_op jit(solution)/shard_map/while/body/eval_jaxpr/ppermute | solution.py:16
  220.3 5.5 %collective-permute-done = bf16[4,128,128]{2,1,0:T(8,128)(2,1)S(1)} collective-permute-done((bf16[4,128,128]{2,1,0:T(8,128)(2,1)S(1)}, bf16[4,128,128]{2,1,0:T(8,128)(2,1)S(1)}, u32[]{:S(2)}, u32[]{:S(2)}) %collective-permute-start) | collective-permute-done | bytes 131104 | tf_op jit(solution)/shard_map/while/body/eval_jaxpr/ppermute | solution.py:16
  228.2 6.1 %collective-permute-done = bf16[4,128,128]{2,1,0:T(8,128)(2,1)S(1)} collective-permute-done((bf16[4,128,128]{2,1,0:T(8,128)(2,1)S(1)}, bf16[4,128,128]{2,1,0:T(8,128)(2,1)S(1)}, u32[]{:S(2)}, u32[]{:S(2)}) %collective-permute-start) | collective-permute-done | bytes 131104 | tf_op jit(solution)/shard_map/while/body/eval_jaxpr/ppermute | solution.py:16
  236.7 6.1 %collective-permute-done = bf16[4,128,128]{2,1,0:T(8,128)(2,1)S(1)} collective-permute-done((bf16[4,128,128]{2,1,0:T(8,128)(2,1)S(1)}, bf16[4,128,128]{2,1,0:T(8,128)(2,1)S(1)}, u32[]{:S(2)}, u32[]{:S(2)}) %collective-permute-start) | collective-permute-done | bytes 131104 | tf_op jit(solution)/shard_map/while/body/eval_jaxpr/ppermute | solution.py:16
  245.3 6.1 %collective-permute-done = bf16[4,128,128]{2,1,0:T(8,128)(2,1)S(1)} collective-permute-done((bf16[4,128,128]{2,1,0:T(8,128)(2,1)S(1)}, bf16[4,128,128]{2,1,0:T(8,128)(2,1)S(1)}, u32[]{:S(2)}, u32[]{:S(2)}) %collective-permute-start) | collective-permute-done | bytes 131104 | tf_op jit(solution)/shard_map/while/body/eval_jaxpr/ppermute | solution.py:16
  253.8 6.7 %collective-permute-done = bf16[4,128,128]{2,1,0:T(8,128)(2,1)S(1)} collective-permute-done((bf16[4,128,128]{2,1,0:T(8,128)(2,1)S(1)}, bf16[4,128,128]{2,1,0:T(8,128)(2,1)S(1)}, u32[]{:S(2)}, u32[]{:S(2)}) %collective-permute-start) | collective-permute-done | bytes 131104 | tf_op jit(solution)/shard_map/while/body/eval_jaxpr/ppermute | solution.py:16
  262.9 7.3 %collective-permute-done = bf16[4,128,128]{2,1,0:T(8,128)(2,1)S(1)} collective-permute-done((bf16[4,128,128]{2,1,0:T(8,128)(2,1)S(1)}, bf16[4,128,128]{2,1,0:T(8,128)(2,1)S(1)}, u32[]{:S(2)}, u32[]{:S(2)}) %collective-permute-start) | collective-permute-done | bytes 131104 | tf_op jit(solution)/shard_map/while/body/eval_jaxpr/ppermute | solution.py:16
  272.6 6.4 %collective-permute-done = bf16[4,128,128]{2,1,0:T(8,128)(2,1)S(1)} collective-permute-done((bf16[4,128,128]{2,1,0:T(8,128)(2,1)S(1)}, bf16[4,128,128]{2,1,0:T(8,128)(2,1)S(1)}, u32[]{:S(2)}, u32[]{:S(2)}) %collective-permute-start) | collective-permute-done | bytes 131104 | tf_op jit(solution)/shard_map/while/body/eval_jaxpr/ppermute | solution.py:16
  281.4 6.1 %collective-permute-done = bf16[4,128,128]{2,1,0:T(8,128)(2,1)S(1)} collective-permute-done((bf16[4,128,128]{2,1,0:T(8,128)(2,1)S(1)}, bf16[4,128,128]{2,1,0:T(8,128)(2,1)S(1)}, u32[]{:S(2)}, u32[]{:S(2)}) %collective-permute-start) | collective-permute-done | bytes 131104 | tf_op jit(solution)/shard_map/while/body/eval_jaxpr/ppermute | solution.py:16
  289.9 6.1 %collective-permute-done = bf16[4,128,128]{2,1,0:T(8,128)(2,1)S(1)} collective-permute-done((bf16[4,128,128]{2,1,0:T(8,128)(2,1)S(1)}, bf16[4,128,128]{2,1,0:T(8,128)(2,1)S(1)}, u32[]{:S(2)}, u32[]{:S(2)}) %collective-permute-start) | collective-permute-done | bytes 131104 | tf_op jit(solution)/shard_map/while/body/eval_jaxpr/ppermute | solution.py:16
  298.4 6.1 %collective-permute-done = bf16[4,128,128]{2,1,0:T(8,128)(2,1)S(1)} collective-permute-done((bf16[4,128,128]{2,1,0:T(8,128)(2,1)S(1)}, bf16[4,128,128]{2,1,0:T(8,128)(2,1)S(1)}, u32[]{:S(2)}, u32[]{:S(2)}) %collective-permute-start) | collective-permute-done | bytes 131104 | tf_op jit(solution)/shard_map/while/body/eval_jaxpr/ppermute | solution.py:16
  307.0 6.1 %collective-permute-done = bf16[4,128,128]{2,1,0:T(8,128)(2,1)S(1)} collective-permute-done((bf16[4,128,128]{2,1,0:T(8,128)(2,1)S(1)}, bf16[4,128,128]{2,1,0:T(8,128)(2,1)S(1)}, u32[]{:S(2)}, u32[]{:S(2)}) %collective-permute-start) | collective-permute-done | bytes 131104 | tf_op jit(solution)/shard_map/while/body/eval_jaxpr/ppermute | solution.py:16
  315.5 6.7 %collective-permute-done = bf16[4,128,128]{2,1,0:T(8,128)(2,1)S(1)} collective-permute-done((bf16[4,128,128]{2,1,0:T(8,128)(2,1)S(1)}, bf16[4,128,128]{2,1,0:T(8,128)(2,1)S(1)}, u32[]{:S(2)}, u32[]{:S(2)}) %collective-permute-start) | collective-permute-done | bytes 131104 | tf_op jit(solution)/shard_map/while/body/eval_jaxpr/ppermute | solution.py:16
  324.7 6.1 %collective-permute-done = bf16[4,128,128]{2,1,0:T(8,128)(2,1)S(1)} collective-permute-done((bf16[4,128,128]{2,1,0:T(8,128)(2,1)S(1)}, bf16[4,128,128]{2,1,0:T(8,128)(2,1)S(1)}, u32[]{:S(2)}, u32[]{:S(2)}) %collective-permute-start) | collective-permute-done | bytes 131104 | tf_op jit(solution)/shard_map/while/body/eval_jaxpr/ppermute | solution.py:16
  333.2 6.1 %collective-permute-done = bf16[4,128,128]{2,1,0:T(8,128)(2,1)S(1)} collective-permute-done((bf16[4,128,128]{2,1,0:T(8,128)(2,1)S(1)}, bf16[4,128,128]{2,1,0:T(8,128)(2,1)S(1)}, u32[]{:S(2)}, u32[]{:S(2)}) %collective-permute-start) | collective-permute-done | bytes 131104 | tf_op jit(solution)/shard_map/while/body/eval_jaxpr/ppermute | solution.py:16
  339.4 9.0 %while.39 = (s32[]{:T(128)}, f32[4,128,128]{2,1,0:T(8,128)S(1)}, f32[4,4,128,128]{3,2,1,0:T(8,128)}, f32[4,4,128,128]{3,2,1,0:T(8,128)}, f32[4,4,128,128]{3,2,1,0:T(8,128)}) while((s32[]{:T(128)}, f32[4,128,128]{2,1,0:T(8,128)S(1)}, f32[4,4,128,128]{3,2,1,0:T(8,128)}, f32[4,4,128,128]{3,2,1,0:T(8,128)}, ...), condition=%wide.region_11.12_spmd.clone, body=%wide.region_10.11_spmd.sunk.clone | while | flops 100728832 | bytes 2098249 | solution.py:154
  357.6 15.3 %all_to_all.5 = bf16[4,64,2048]{2,1,0:T(8,128)(2,1)S(1)} all-to-all(bf16[4,64,2048]{2,1,0:T(8,128)(2,1)S(1)} %bitcast.107), channel_id=1, replica_groups=mesh['parts'=2,'seq'=16,'head'=4,'rep'=2] {'head'}, dimensions={0} | all-to-all | bytes 2097152 | tf_op jit(solution)/shard_map/all_to_all | solution.py:27
  (172 shorter events, 92.1 us)
Async XLA Ops:
  0.0 356.8 %copy-start = (bf16[512,2048]{1,0:T(8,128)(2,1)S(1)}, bf16[512,2048]{1,0:T(8,128)(2,1)}, u32[]{:S(2)}) copy-start(bf16[512,2048]{1,0:T(8,128)(2,1)} %param.21) | copy-start | bytes 6291460
  0.0 13.1 %copy-start.12 = (bf16[1,256,512]{2,1,0:T(8,128)(2,1)S(1)}, bf16[1,256,512]{2,1,0:T(8,128)(2,1)}, u32[]{:S(2)}) copy-start(bf16[1,256,512]{2,1,0:T(8,128)(2,1)} %param.14) | copy-start | bytes 786436
  20.8 163.1 %copy-start.11 = (bf16[1,256,2,512]{3,2,1,0:T(2,128)(2,1)S(1)}, bf16[1,256,2,512]{3,2,1,0:T(2,128)(2,1)}, u32[]{:S(2)}) copy-start(bf16[1,256,2,512]{3,2,1,0:T(2,128)(2,1)} %param.16) | copy-start | bytes 1572868
  25.2 162.0 %copy-start.17 = (f32[4,4,128]{2,1,0:T(4,128)S(1)}, f32[4,4,128]{2,1,0:T(4,128)}, u32[]{:S(2)}) copy-start(f32[4,4,128]{2,1,0:T(4,128)} %get-tuple-element.147) | copy-start | bytes 24580
  190.4 6.5 %copy-start.4 = (f32[4,4,128,256]{3,2,1,0:T(8,128)}, f32[4,4,128,256]{3,2,1,0:T(8,128)S(1)}, u32[]{:S(2)}) copy-start(f32[4,4,128,256]{3,2,1,0:T(8,128)S(1)} %fusion.19) | copy-start | bytes 6291460
  208.8 8.4 %collective-permute-start = (bf16[4,128,128]{2,1,0:T(8,128)(2,1)S(1)}, bf16[4,128,128]{2,1,0:T(8,128)(2,1)S(1)}, u32[]{:S(2)}, u32[]{:S(2)}) collective-permute-start(bf16[4,128,128]{2,1,0:T(8,128)(2,1)S(1)} %fusion.89), channel_id=1, source_target_pairs={{0,8},{8,16},{16,24},{24,32},{32,40},{40,48},{48,56},{56,64},{64,7... | collective-permute-start | bytes 393224 | tf_op jit(solution)/shard_map/while/body/eval_jaxpr/ppermute | solution.py:16
  217.7 8.1 %collective-permute-start = (bf16[4,128,128]{2,1,0:T(8,128)(2,1)S(1)}, bf16[4,128,128]{2,1,0:T(8,128)(2,1)S(1)}, u32[]{:S(2)}, u32[]{:S(2)}) collective-permute-start(bf16[4,128,128]{2,1,0:T(8,128)(2,1)S(1)} %fusion.89), channel_id=1, source_target_pairs={{0,8},{8,16},{16,24},{24,32},{32,40},{40,48},{48,56},{56,64},{64,7... | collective-permute-start | bytes 393224 | tf_op jit(solution)/shard_map/while/body/eval_jaxpr/ppermute | solution.py:16
  226.2 8.1 %collective-permute-start = (bf16[4,128,128]{2,1,0:T(8,128)(2,1)S(1)}, bf16[4,128,128]{2,1,0:T(8,128)(2,1)S(1)}, u32[]{:S(2)}, u32[]{:S(2)}) collective-permute-start(bf16[4,128,128]{2,1,0:T(8,128)(2,1)S(1)} %fusion.89), channel_id=1, source_target_pairs={{0,8},{8,16},{16,24},{24,32},{32,40},{40,48},{48,56},{56,64},{64,7... | collective-permute-start | bytes 393224 | tf_op jit(solution)/shard_map/while/body/eval_jaxpr/ppermute | solution.py:16
  234.8 8.1 %collective-permute-start = (bf16[4,128,128]{2,1,0:T(8,128)(2,1)S(1)}, bf16[4,128,128]{2,1,0:T(8,128)(2,1)S(1)}, u32[]{:S(2)}, u32[]{:S(2)}) collective-permute-start(bf16[4,128,128]{2,1,0:T(8,128)(2,1)S(1)} %fusion.89), channel_id=1, source_target_pairs={{0,8},{8,16},{16,24},{24,32},{32,40},{40,48},{48,56},{56,64},{64,7... | collective-permute-start | bytes 393224 | tf_op jit(solution)/shard_map/while/body/eval_jaxpr/ppermute | solution.py:16
  243.3 8.1 %collective-permute-start = (bf16[4,128,128]{2,1,0:T(8,128)(2,1)S(1)}, bf16[4,128,128]{2,1,0:T(8,128)(2,1)S(1)}, u32[]{:S(2)}, u32[]{:S(2)}) collective-permute-start(bf16[4,128,128]{2,1,0:T(8,128)(2,1)S(1)} %fusion.89), channel_id=1, source_target_pairs={{0,8},{8,16},{16,24},{24,32},{32,40},{40,48},{48,56},{56,64},{64,7... | collective-permute-start | bytes 393224 | tf_op jit(solution)/shard_map/while/body/eval_jaxpr/ppermute | solution.py:16
  251.9 8.6 %collective-permute-start = (bf16[4,128,128]{2,1,0:T(8,128)(2,1)S(1)}, bf16[4,128,128]{2,1,0:T(8,128)(2,1)S(1)}, u32[]{:S(2)}, u32[]{:S(2)}) collective-permute-start(bf16[4,128,128]{2,1,0:T(8,128)(2,1)S(1)} %fusion.89), channel_id=1, source_target_pairs={{0,8},{8,16},{16,24},{24,32},{32,40},{40,48},{48,56},{56,64},{64,7... | collective-permute-start | bytes 393224 | tf_op jit(solution)/shard_map/while/body/eval_jaxpr/ppermute | solution.py:16
  260.9 9.2 %collective-permute-start = (bf16[4,128,128]{2,1,0:T(8,128)(2,1)S(1)}, bf16[4,128,128]{2,1,0:T(8,128)(2,1)S(1)}, u32[]{:S(2)}, u32[]{:S(2)}) collective-permute-start(bf16[4,128,128]{2,1,0:T(8,128)(2,1)S(1)} %fusion.89), channel_id=1, source_target_pairs={{0,8},{8,16},{16,24},{24,32},{32,40},{40,48},{48,56},{56,64},{64,7... | collective-permute-start | bytes 393224 | tf_op jit(solution)/shard_map/while/body/eval_jaxpr/ppermute | solution.py:16
  270.6 8.4 %collective-permute-start = (bf16[4,128,128]{2,1,0:T(8,128)(2,1)S(1)}, bf16[4,128,128]{2,1,0:T(8,128)(2,1)S(1)}, u32[]{:S(2)}, u32[]{:S(2)}) collective-permute-start(bf16[4,128,128]{2,1,0:T(8,128)(2,1)S(1)} %fusion.89), channel_id=1, source_target_pairs={{0,8},{8,16},{16,24},{24,32},{32,40},{40,48},{48,56},{56,64},{64,7... | collective-permute-start | bytes 393224 | tf_op jit(solution)/shard_map/while/body/eval_jaxpr/ppermute | solution.py:16
  279.4 8.1 %collective-permute-start = (bf16[4,128,128]{2,1,0:T(8,128)(2,1)S(1)}, bf16[4,128,128]{2,1,0:T(8,128)(2,1)S(1)}, u32[]{:S(2)}, u32[]{:S(2)}) collective-permute-start(bf16[4,128,128]{2,1,0:T(8,128)(2,1)S(1)} %fusion.89), channel_id=1, source_target_pairs={{0,8},{8,16},{16,24},{24,32},{32,40},{40,48},{48,56},{56,64},{64,7... | collective-permute-start | bytes 393224 | tf_op jit(solution)/shard_map/while/body/eval_jaxpr/ppermute | solution.py:16
  287.9 8.1 %collective-permute-start = (bf16[4,128,128]{2,1,0:T(8,128)(2,1)S(1)}, bf16[4,128,128]{2,1,0:T(8,128)(2,1)S(1)}, u32[]{:S(2)}, u32[]{:S(2)}) collective-permute-start(bf16[4,128,128]{2,1,0:T(8,128)(2,1)S(1)} %fusion.89), channel_id=1, source_target_pairs={{0,8},{8,16},{16,24},{24,32},{32,40},{40,48},{48,56},{56,64},{64,7... | collective-permute-start | bytes 393224 | tf_op jit(solution)/shard_map/while/body/eval_jaxpr/ppermute | solution.py:16
  296.5 8.1 %collective-permute-start = (bf16[4,128,128]{2,1,0:T(8,128)(2,1)S(1)}, bf16[4,128,128]{2,1,0:T(8,128)(2,1)S(1)}, u32[]{:S(2)}, u32[]{:S(2)}) collective-permute-start(bf16[4,128,128]{2,1,0:T(8,128)(2,1)S(1)} %fusion.89), channel_id=1, source_target_pairs={{0,8},{8,16},{16,24},{24,32},{32,40},{40,48},{48,56},{56,64},{64,7... | collective-permute-start | bytes 393224 | tf_op jit(solution)/shard_map/while/body/eval_jaxpr/ppermute | solution.py:16
  305.0 8.1 %collective-permute-start = (bf16[4,128,128]{2,1,0:T(8,128)(2,1)S(1)}, bf16[4,128,128]{2,1,0:T(8,128)(2,1)S(1)}, u32[]{:S(2)}, u32[]{:S(2)}) collective-permute-start(bf16[4,128,128]{2,1,0:T(8,128)(2,1)S(1)} %fusion.89), channel_id=1, source_target_pairs={{0,8},{8,16},{16,24},{24,32},{32,40},{40,48},{48,56},{56,64},{64,7... | collective-permute-start | bytes 393224 | tf_op jit(solution)/shard_map/while/body/eval_jaxpr/ppermute | solution.py:16
  313.6 8.7 %collective-permute-start = (bf16[4,128,128]{2,1,0:T(8,128)(2,1)S(1)}, bf16[4,128,128]{2,1,0:T(8,128)(2,1)S(1)}, u32[]{:S(2)}, u32[]{:S(2)}) collective-permute-start(bf16[4,128,128]{2,1,0:T(8,128)(2,1)S(1)} %fusion.89), channel_id=1, source_target_pairs={{0,8},{8,16},{16,24},{24,32},{32,40},{40,48},{48,56},{56,64},{64,7... | collective-permute-start | bytes 393224 | tf_op jit(solution)/shard_map/while/body/eval_jaxpr/ppermute | solution.py:16
  322.7 8.1 %collective-permute-start = (bf16[4,128,128]{2,1,0:T(8,128)(2,1)S(1)}, bf16[4,128,128]{2,1,0:T(8,128)(2,1)S(1)}, u32[]{:S(2)}, u32[]{:S(2)}) collective-permute-start(bf16[4,128,128]{2,1,0:T(8,128)(2,1)S(1)} %fusion.89), channel_id=1, source_target_pairs={{0,8},{8,16},{16,24},{24,32},{32,40},{40,48},{48,56},{56,64},{64,7... | collective-permute-start | bytes 393224 | tf_op jit(solution)/shard_map/while/body/eval_jaxpr/ppermute | solution.py:16
  331.3 8.1 %collective-permute-start = (bf16[4,128,128]{2,1,0:T(8,128)(2,1)S(1)}, bf16[4,128,128]{2,1,0:T(8,128)(2,1)S(1)}, u32[]{:S(2)}, u32[]{:S(2)}) collective-permute-start(bf16[4,128,128]{2,1,0:T(8,128)(2,1)S(1)} %fusion.89), channel_id=1, source_target_pairs={{0,8},{8,16},{16,24},{24,32},{32,40},{40,48},{48,56},{56,64},{64,7... | collective-permute-start | bytes 393224 | tf_op jit(solution)/shard_map/while/body/eval_jaxpr/ppermute | solution.py:16
  348.4 3.3 copy-start.6
  348.4 4.4 %copy-start.3 = (f32[4,4,64,2,128]{4,3,2,1,0:T(2,128)S(1)}, f32[4,4,64,2,128]{4,3,2,1,0:T(2,128)}, u32[]{:S(2)}) copy-start(f32[4,4,64,2,128]{4,3,2,1,0:T(2,128)} %copy-done.1) | copy-start | bytes 3145732
  348.4 4.4 %copy-start.9 = (f32[4,4,64,128]{3,2,1,0:T(8,128)S(1)}, f32[4,4,64,128]{3,2,1,0:T(8,128)}, u32[]{:S(2)}) copy-start(f32[4,4,64,128]{3,2,1,0:T(8,128)} %slice.31) | copy-start | bytes 1572868
  352.8 3.4 copy-start.21
  (13 other events, 26.2 us)
where the time goes:
time: 377 us; the launch traced here: 374 us
  other arithmetic  170 us (45%)
  waiting for transfers between devices  92.5 us (25%)
  matrix products  43 us (11%)
  starting transfers between devices  31.8 us (8%)
  local copies, waits for them, and re-layouts  19.7 us (5%)
  blocking collectives  15.3 us (4%)
    another operation x2, other arithmetic, block_parts(): lax.linalg.triangular_solve(system, right_side, left_side=True, lower=Tru...  159 us
    ppermute x15, waiting for transfers between devices, shifted(): lax.ppermute(value, axis, [(source, source + steps) for source in range(i...  92.5 us
    ppermute x15, starting transfers between devices, shifted(): lax.ppermute(value, axis, [(source, source + steps) for source in range(i...  31.8 us
    dot_general x27, matrix products, heads_product(): return jnp.einsum('hij,hjk->hik', left_maps, right_maps, precision=highest)  22.7 us
    all_to_all x1, blocking collectives, summed_on_arrival(): lax.all_to_all(parts, axis, split_axis=0, concat_axis=0, tiled=True)  15.3 us
  transfers between devices with their start and end apart: 15, of which 15 were waited for; matrix products, arithmetic and copies ran while one was open for 0% of the time, Pallas kernels for 0%

commit v1 on v0

v1 whole, which is shorter than its diff:
```python
import functools

import jax
import jax.numpy as jnp
from jax import lax
from jax.experimental import pallas as pl
from jax.experimental.pallas import tpu as pltpu
from jax.sharding import PartitionSpec as P

BLOCK = 64
LONGEST = 2048
EPS = 1e-06
FAR = -1e30
MESH = pl.DeviceIdType.MESH
f32 = jnp.float32
bf16 = jnp.bfloat16


def mm(a, b):
    return lax.dot_general(a, b, (((1,), (0,)), ((), ())), preferred_element_type=f32)


def mm_t(a, b):
    return lax.dot_general(a, b, (((1,), (1,)), ((), ())), preferred_element_type=f32)


def split(x):
    hi = x.astype(bf16)
    return hi, (x - hi.astype(f32)).astype(bf16)


def iota(shape, dim):
    return lax.broadcasted_iota(jnp.int32, shape, dim)


def exact(a, b):
    return lax.dot_general(
        a, b, (((1,), (0,)), ((), ())), preferred_element_type=f32, precision=lax.Precision.HIGHEST
    )


def seg_of(pos, ends):
    total = jnp.zeros_like(pos)
    for end in ends:
        total = total + (pos >= end).astype(jnp.int32)
    return total


def rows_of(gate, beta, refl):
    tokens = gate.shape[1]
    subs = tokens * refl
    t, r = iota((tokens, subs), 0), iota((tokens, subs), 1) // refl
    upto = ((t <= r) & (t // BLOCK == r // BLOCK)).astype(f32)
    src, dst = iota((subs, subs), 0), iota((subs, subs), 1)
    place = (dst == (src % tokens) * refl + src // tokens).astype(f32)
    t2, r2 = iota((tokens, tokens), 0), iota((tokens, tokens), 1)
    upto_token = ((t2 <= r2) & (t2 // BLOCK == r2 // BLOCK)).astype(f32)
    return exact(gate, upto), exact(beta, place), exact(gate, upto_token)


def block_masks(offset, ends, block, refl):
    n = refl * BLOCK
    start = offset + block * BLOCK
    before = sum((start - 1 >= e).astype(jnp.int32) for e in ends)
    before = jnp.where(start == 0, -1, before)
    last = sum((start + BLOCK - 1 >= e).astype(jnp.int32) for e in ends)
    seg_row = seg_of(start + iota((1, n), 1) // refl, ends)
    seg_col = seg_of(start + iota((n, 1), 0) // refl, ends)
    seg_tok = seg_of(start + iota((BLOCK, 1), 0), ends)
    i, j = iota((n, n), 0), iota((n, n), 1)
    pair = jnp.where((i >= j) & (seg_col == seg_row), 0.0, FAR)
    ti, tj = iota((BLOCK, n), 0), iota((BLOCK, n), 1)
    read = jnp.where((ti >= tj // refl) & (seg_tok == seg_row), 0.0, FAR)
    carry_row = jnp.where(seg_row == before, 0.0, FAR)
    carry_tok = jnp.where(seg_tok == before, 0.0, FAR)
    end_col = jnp.where(seg_col == last, 0.0, FAR)
    return pair, read, carry_row, carry_tok, end_col


def level_mask(n, level):
    i, j = iota((n, n), 0), iota((n, n), 1)
    return ((i > j) & (lax.shift_right_logical(i ^ j, level) == 1)).astype(f32).astype(bf16)


def levels_of(n):
    return n.bit_length() - 1


def head_maps(blocks, masks, eye, levels):
    n = eye.shape[0]
    width = blocks[0][0].shape[1]
    scale = width**-0.5
    eye16 = eye.astype(bf16)
    grams, lowers, xs, norms = [], [], [], []
    for (k, v, q, c_row, c_col, b_row, b_col, ct_col), (pair, *_) in zip(blocks, masks):
        both = mm_t(jnp.concatenate([k, q], axis=0), k)
        gram, qk = both[:n], both[n:]
        diag = gram * eye
        n_row = lax.rsqrt(jnp.sum(diag, axis=0, keepdims=True) + EPS)
        n_col = lax.rsqrt(jnp.sum(diag, axis=1, keepdims=True) + EPS)
        ratio = jnp.exp((c_col - c_row) + pair)
        lower = ((b_col * n_col) * ratio) * (n_row * gram)
        lower = lower - lower * eye
        grams.append(qk)
        norms.append((n_row, n_col))
        lowers.append(split(lower))
    xs = [eye16 - low[0] * levels(0) for low in lowers]
    for level in range(1, levels_of(n)):
        mask = levels(level)
        ys = [mm(low[0] * mask, x).astype(bf16) for low, x in zip(lowers, xs)]
        xs = [x - mm(x, y).astype(bf16) for x, y in zip(xs, ys)]
    outs = []
    lefts = [
        mm(jnp.concatenate(low, axis=1), jnp.concatenate([x, x], axis=0))
        for low, x in zip(lowers, xs)
    ]
    rests = [((eye - x.astype(f32)) - left).astype(bf16) for x, left in zip(xs, lefts)]
    invs = [x.astype(f32) + mm(x, rest) for x, rest in zip(xs, rests)]
    values, keys = [], []
    for inv, (k, v, q, c_row, c_col, b_row, b_col, ct_col), m, (n_row, n_col) in zip(
        invs, blocks, masks, norms
    ):
        carry_row = jnp.exp(c_row + m[2])
        for_value = inv * b_row
        for_key = inv * (b_row * carry_row * n_row)
        values.append(
            mm(jnp.concatenate(split(for_value), axis=1), jnp.concatenate([v, v], axis=0))
        )
        keys.append(mm(jnp.concatenate(split(for_key), axis=1), jnp.concatenate([k, k], axis=0)))
    maps, reads = [], []
    for wv, wk, qk, (k, v, q, c_row, c_col, b_row, b_col, ct_col), m, (n_row, n_col) in zip(
        values, keys, grams, blocks, masks, norms
    ):
        both = jnp.concatenate([wv, wk], axis=1)
        c_last = c_row[:, n - 1 :]
        end = jnp.exp((c_last - c_col) + m[4]) * n_col
        hi, lo = split(both * end)
        kt = jnp.transpose(k)
        ew = mm(jnp.concatenate([kt, kt], axis=1), jnp.concatenate([hi, lo], axis=0))
        carry_last = jnp.exp(c_last + m[2][:, n - 1 :])
        maps.append((carry_last * eye - ew[:, width:], ew[:, :width]))
        qf = q.astype(f32)
        nq = lax.rsqrt(jnp.sum(qf * qf, axis=1, keepdims=True) + EPS) * scale
        weights = jnp.exp((ct_col - c_row) + m[1]) * nq * (n_row * qk)
        got = mm(weights.astype(bf16), both.astype(bf16))
        carry_tok = jnp.exp(ct_col + m[3])
        reads.append(((carry_tok * nq) * qf - got[:, width:], got[:, :width]))
    total = jnp.concatenate(maps[0], axis=1)
    g_rows, o_rows = [reads[0][0].astype(bf16)], [reads[0][1]]
    for (map_b, add_b), (qeff, o) in zip(maps[1:], reads[1:]):
        hi, lo = split(total)
        m_hi, m_lo = split(map_b)
        q16 = qeff.astype(bf16)
        left = jnp.concatenate(
            [
                jnp.concatenate([m_hi, m_lo], axis=1),
                jnp.concatenate([q16, jnp.zeros_like(q16)], axis=1),
            ],
            axis=0,
        )
        wide = mm(left, jnp.concatenate([hi, hi], axis=0))
        total = wide[:n] + mm(m_hi, lo)
        total = jnp.concatenate([total[:, :width], total[:, width:] + add_b], axis=1)
        g_rows.append(wide[n:, :width].astype(bf16))
        o_rows.append(o + wide[n:, width:])
    return total[:, :width], total[:, width:], g_rows, o_rows


def kernel(
    n_seq,
    n_head,
    rounds,
    q_hbm,
    k_hbm,
    v_hbm,
    beta_ref,
    gate_ref,
    len_ref,
    gain_ref,
    w_hbm,
    out_ref,
    q_s,
    k_s,
    v_s,
    w_s,
    row_s,
    col_c,
    col_b,
    col_t,
    pair_s,
    read_s,
    crow_s,
    ctok_s,
    ecol_s,
    eye_s,
    lev_s,
    map_s,
    add_s,
    g_s,
    o_s,
    send_s,
    recv_s,
    norm_s,
    part_s,
    got_s,
    in_sem,
    w_sem,
    ring_send,
    ring_recv,
    x_send,
    x_recv,
):
    z = lax.axis_index("seq")
    x = lax.axis_index("head")
    heads, subs, width = k_s.shape
    tokens = q_s.shape[1]
    refl = subs // tokens
    blocks = tokens // BLOCK
    n = refl * BLOCK
    ahead, behind = lax.rem(z + 1, n_seq), lax.rem(z + n_seq - 1, n_seq)

    barrier = pltpu.get_barrier_semaphore()
    pl.semaphore_signal(barrier, inc=1, device_id={"seq": ahead}, device_id_type=MESH)
    pl.semaphore_signal(barrier, inc=1, device_id={"seq": behind}, device_id_type=MESH)
    for o in range(1, n_head):
        pl.semaphore_signal(
            barrier, inc=1, device_id={"head": lax.rem(x + o, n_head)}, device_id_type=MESH
        )

    k_rows = k_hbm.reshape(subs, heads * width)
    v_rows = v_hbm.reshape(subs, heads * width)

    def loads(h):
        lanes = pl.ds(pl.multiple_of(h * width, width), width)
        return (
            pltpu.make_async_copy(k_rows.at[:, lanes], k_s.at[h], in_sem.at[0, h]),
            pltpu.make_async_copy(v_rows.at[:, lanes], v_s.at[h], in_sem.at[1, h]),
            pltpu.make_async_copy(q_hbm.at[:, lanes], q_s.at[h], in_sem.at[2, h]),
        )

    for h in range(heads):
        for copy in loads(h):
            copy.start()
    w_copy = pltpu.make_async_copy(w_hbm, w_s, w_sem)
    w_copy.start()

    offset = z * tokens
    ends, run = [], 0
    for i in range(len_ref.shape[0]):
        run = run + len_ref[i]
        ends.append(run)
    beta = jnp.concatenate([beta_ref[j] for j in range(refl)], axis=1)
    c_exp, b_exp, c_tok = rows_of(gate_ref[...], beta, refl)
    rows = jnp.concatenate([c_exp, b_exp], axis=0)
    for i in range(2 * heads):
        row_s[i] = rows[i : i + 1]
    cols = jnp.transpose(rows)
    cols_t = jnp.transpose(jnp.concatenate([c_tok, c_tok], axis=0))
    for h in range(heads):
        col_c[h] = cols[:, h : h + 1]
        col_b[h] = cols[:, heads + h : heads + h + 1]
        col_t[h] = cols_t[:, h : h + 1]
    for b in range(blocks):
        pair_s[b], read_s[b], crow_s[b], ctok_s[b], ecol_s[b] = block_masks(offset, ends, b, refl)
    eye_s[...] = (iota((n, n), 0) == iota((n, n), 1)).astype(f32)
    for level in range(levels_of(n)):
        lev_s[level] = level_mask(n, level)

    def hop(r, h):
        return pltpu.make_async_remote_copy(
            src_ref=send_s.at[r, h],
            dst_ref=recv_s.at[r, h],
            send_sem=ring_send.at[r, h],
            recv_sem=ring_recv.at[r, h],
            device_id={"seq": ahead},
            device_id_type=MESH,
        )

    def step(r, h):
        hop(r - 1, h).wait_recv()
        got = recv_s[r - 1, h]
        state = add_s[h] + mm(map_s[h], jnp.concatenate([got, got], axis=0))
        send_s[r, h] = state.astype(bf16)
        hop(r, h).start()

    def one_head(h, carry):
        for copy in loads(h):
            copy.wait()
        data, masks = [], []
        for b in range(blocks):
            subs_b, toks_b = pl.ds(b * n, n), pl.ds(b * BLOCK, BLOCK)
            data.append(
                (
                    k_s[h, subs_b, :],
                    v_s[h, subs_b, :],
                    q_s[h, toks_b, :],
                    row_s[h, :, subs_b],
                    col_c[h, subs_b, :],
                    row_s[heads + h, :, subs_b],
                    col_b[h, subs_b, :],
                    col_t[h, toks_b, :],
                )
            )
            masks.append((pair_s[b], read_s[b], crow_s[b], ctok_s[b], ecol_s[b]))
        total, add, g_rows, o_rows = head_maps(data, masks, eye_s[...], lambda l: lev_s[l])
        map_s[h] = jnp.concatenate(split(total), axis=1)
        add_s[h] = add
        for b in range(blocks):
            g_s[h, pl.ds(b * BLOCK, BLOCK), :] = g_rows[b]
            o_s[h, pl.ds(b * BLOCK, BLOCK), :] = o_rows[b]

        @pl.when(h == 0)
        def _():
            pl.semaphore_wait(barrier, n_head + 1)

        send_s[0, h] = add.astype(bf16)
        hop(0, h).start()

        def earlier(e, c):
            step(h - e, e)
            return c

        lax.fori_loop(0, h, earlier, 0)
        return carry

    lax.fori_loop(0, heads, one_head, 0)

    for wave in range(heads, rounds - 1 + heads):
        for h in range(heads):
            r = wave - h
            if 1 <= r < rounds:
                step(r, h)

    w_copy.wait()
    for h in range(heads):
        hop(rounds - 1, h).wait_recv()
        out = o_s[h] + mm(g_s[h], recv_s[rounds - 1, h])
        mean = jnp.sum(out * out, axis=1, keepdims=True) * (1.0 / width)
        norm_s[:, h * width : (h + 1) * width] = (
            out * lax.rsqrt(mean + EPS) * gain_ref[...]
        ).astype(bf16)

    chunks = part_s.shape[0]
    cols_n = part_s.shape[2]
    share = out_ref.shape[0]

    def give(o, c):
        dest = lax.rem(x + o, n_head)
        return pltpu.make_async_remote_copy(
            src_ref=part_s.at[c, pl.ds(pl.multiple_of(dest * share, share), share), :],
            dst_ref=got_s.at[o - 1, c],
            send_sem=x_send.at[o - 1, c],
            recv_sem=x_recv.at[o - 1, c],
            device_id={"head": dest},
            device_id_type=MESH,
        )

    normed = norm_s[...]
    for c in range(chunks):
        part_s[c] = mm(normed, w_s[:, c * cols_n : (c + 1) * cols_n]).astype(bf16)
        for o in (2, 1, 3):
            give(o, c).start()
    own = pl.ds(pl.multiple_of(x * share, share), share)
    for c in range(chunks):
        total = part_s[c, own, :].astype(f32)
        for o in (1, 3, 2):
            give(o, c).wait_recv()
            total = total + got_s[o - 1, c].astype(f32)
        out_ref[:, c * cols_n : (c + 1) * cols_n] = total.astype(bf16)

    def drain(r, c):
        for h in range(heads):
            hop(r, h).wait_send()
        return c

    lax.fori_loop(0, rounds, drain, 0)
    for c in range(chunks):
        for o in range(1, n_head):
            give(o, c).wait_send()


def solution(mesh):
    n_seq, n_head = mesh.shape["seq"], mesh.shape["head"]

    def body(queries, keys, values, beta, gate, lengths, gain, weight):
        tokens, lanes = queries.shape[1:]
        refl, heads = beta.shape[2:]
        width = lanes // heads
        subs = tokens * refl
        blocks = tokens // BLOCK
        n = refl * BLOCK
        model = weight.shape[1]
        share = tokens // n_head
        rounds = min(n_seq - 1, -(-LONGEST // tokens))
        chunks = 4
        hbm = pl.BlockSpec(memory_space=pl.ANY)
        vmem = pl.BlockSpec(memory_space=pltpu.VMEM)
        smem = pl.BlockSpec(memory_space=pltpu.SMEM)
        out = pl.pallas_call(
            functools.partial(kernel, n_seq, n_head, rounds),
            out_shape=jax.ShapeDtypeStruct((share, model), bf16),
            in_specs=[hbm, hbm, hbm, vmem, vmem, smem, vmem, hbm],
            out_specs=vmem,
            scratch_shapes=[
                pltpu.VMEM((heads, tokens, width), bf16),
                pltpu.VMEM((heads, subs, width), bf16),
                pltpu.VMEM((heads, subs, width), bf16),
                pltpu.VMEM((lanes, model), bf16),
                pltpu.VMEM((2 * heads, 1, subs), f32),
                pltpu.VMEM((heads, subs, 1), f32),
                pltpu.VMEM((heads, subs, 1), f32),
                pltpu.VMEM((heads, tokens, 1), f32),
                pltpu.VMEM((blocks, n, n), f32),
                pltpu.VMEM((blocks, BLOCK, n), f32),
                pltpu.VMEM((blocks, 1, n), f32),
                pltpu.VMEM((blocks, BLOCK, 1), f32),
                pltpu.VMEM((blocks, n, 1), f32),
                pltpu.VMEM((n, n), f32),
                pltpu.VMEM((levels_of(n), n, n), bf16),
                pltpu.VMEM((heads, width, 2 * width), bf16),
                pltpu.VMEM((heads, width, width), f32),
                pltpu.VMEM((heads, tokens, width), bf16),
                pltpu.VMEM((heads, tokens, width), f32),
                pltpu.VMEM((rounds, heads, width, width), bf16),
                pltpu.VMEM((rounds, heads, width, width), bf16),
                pltpu.VMEM((tokens, lanes), bf16),
                pltpu.VMEM((chunks, tokens, model // chunks), bf16),
                pltpu.VMEM((n_head - 1, chunks, share, model // chunks), bf16),
                pltpu.SemaphoreType.DMA((3, heads)),
                pltpu.SemaphoreType.DMA,
                pltpu.SemaphoreType.DMA((rounds, heads)),
                pltpu.SemaphoreType.DMA((rounds, heads)),
                pltpu.SemaphoreType.DMA((n_head - 1, chunks)),
                pltpu.SemaphoreType.DMA((n_head - 1, chunks)),
            ],
            compiler_params=pltpu.CompilerParams(
                collective_id=0, has_side_effects=True, vmem_limit_bytes=48 * 1024 * 1024
            ),
        )(
            queries[0],
            keys[0],
            values[0],
            jnp.transpose(beta[0], (1, 2, 0)),
            jnp.transpose(gate[0], (1, 0)),
            lengths[0],
            gain[None, :],
            weight,
        )
        return out[None]

    packs = ("parts", "rep")
    in_specs = (
        P(packs, "seq", "head"),
        P(packs, "seq", None, "head"),
        P(packs, "seq", None, "head"),
        P(packs, "seq", None, "head"),
        P(packs, "seq", "head"),
        P(packs, None),
        P(),
        P("head", None),
    )
    out_specs = P(packs, ("seq", "head"), None)
    return jax.shard_map(body, mesh=mesh, in_specs=in_specs, out_specs=out_specs, check_vma=False)
```

time: 377 us -> 84.9 us (0.23)
  the two profiles are of different devices: /device:TPU:1056 before, /device:TPU:40 now
where the time goes in v1:
time: 84.9 us; the launch traced here: 84.6 us
  Pallas kernels  76.6 us (90%)
  local copies, waits for them, and re-layouts  8.02 us (9%)
    pallas_call x1, Pallas kernels, body(): pl.pallas_call(functools.partial(kernel, n_seq, n_head, rounds), out_shap...  76.6 us
    unnamed x17, local copies, waits for them, and re-layouts  8.02 us

profile of v1, /device:TPU:40, one launch (start us, length us, event | category | flops | bytes accessed | tf_op | source)
XLA Modules:
  0.0 84.6 jit_solution(9628430844904581645)
XLA Ops:
  0.0 0.0 copy-start
  0.0 1.6 %copy-done = bf16[512,2048]{1,0:T(8,128)(2,1)S(1)} copy-done((bf16[512,2048]{1,0:T(8,128)(2,1)S(1)}, bf16[512,2048]{1,0:T(8,128)(2,1)}, u32[]{:S(2)}) %copy-start) | copy-done | bytes 2097176
  1.6 0.0 copy-start.1
  1.6 1.0 %copy-done.1 = bf16[1,256,2,512]{3,2,1,0:T(2,128)(2,1)S(1)} copy-done((bf16[1,256,2,512]{3,2,1,0:T(2,128)(2,1)S(1)}, bf16[1,256,2,512]{3,2,1,0:T(2,128)(2,1)}, u32[]{:S(2)}) %copy-start.1) | copy-done | bytes 524312
  2.6 0.0 copy-start.2
  2.6 1.0 %copy-done.2 = bf16[1,256,2,512]{3,2,1,0:T(2,128)(2,1)S(1)} copy-done((bf16[1,256,2,512]{3,2,1,0:T(2,128)(2,1)S(1)}, bf16[1,256,2,512]{3,2,1,0:T(2,128)(2,1)}, u32[]{:S(2)}) %copy-start.2) | copy-done | bytes 524312
  3.7 0.0 copy-start.3
  3.7 0.9 %copy-done.3 = bf16[1,256,512]{2,1,0:T(8,128)(2,1)S(1)} copy-done((bf16[1,256,512]{2,1,0:T(8,128)(2,1)S(1)}, bf16[1,256,512]{2,1,0:T(8,128)(2,1)}, u32[]{:S(2)}) %copy-start.3) | copy-done | bytes 262168
  4.6 0.0 copy-start.4
  4.6 0.7 copy-done.4
  5.3 0.0 copy-start.5
  5.3 0.7 copy-done.5
  6.0 0.0 copy-start.6
  6.0 0.7 copy-done.6
  6.7 0.0 copy-start.7
  6.7 0.7 copy-done.7
  7.3 76.6 %shard_map.82 = bf16[64,2048]{1,0:T(8,128)(2,1)S(1)} custom-call(bf16[256,512]{1,0:T(8,128)(2,1)S(1)} %bitcast.15, bf16[256,2,512]{2,1,0:T(2,128)(2,1)S(1)} %bitcast.13, bf16[256,2,512]{2,1,0:T(2,128)(2,1)S(1)} %bitcast.14, f32[2,4,256]{2,1,0:T(4,128)S(1)} %bitcast.16, f32[4,256]{1,0:T(4,128)S(1)} %bitcast.17, s32[6]{0:T(128)S(1)} %bitcast.18, ...), custom_call_target="tpu_custom_call" | custom-call | tf_op jit(solution)/shard_map/pallas_call | solution.py:399
  83.9 0.7 copy.10
Async XLA Ops:
  0.0 1.6 %copy-start = (bf16[512,2048]{1,0:T(8,128)(2,1)S(1)}, bf16[512,2048]{1,0:T(8,128)(2,1)}, u32[]{:S(2)}) copy-start(bf16[512,2048]{1,0:T(8,128)(2,1)} %w_hbm.1) | copy-start | bytes 6291460
  1.6 1.0 %copy-start.1 = (bf16[1,256,2,512]{3,2,1,0:T(2,128)(2,1)S(1)}, bf16[1,256,2,512]{3,2,1,0:T(2,128)(2,1)}, u32[]{:S(2)}) copy-start(bf16[1,256,2,512]{3,2,1,0:T(2,128)(2,1)} %param.9) | copy-start | bytes 1572868
  2.6 1.0 %copy-start.2 = (bf16[1,256,2,512]{3,2,1,0:T(2,128)(2,1)S(1)}, bf16[1,256,2,512]{3,2,1,0:T(2,128)(2,1)}, u32[]{:S(2)}) copy-start(bf16[1,256,2,512]{3,2,1,0:T(2,128)(2,1)} %param.10) | copy-start | bytes 1572868
  3.7 0.9 %copy-start.3 = (bf16[1,256,512]{2,1,0:T(8,128)(2,1)S(1)}, bf16[1,256,512]{2,1,0:T(8,128)(2,1)}, u32[]{:S(2)}) copy-start(bf16[1,256,512]{2,1,0:T(8,128)(2,1)} %param.8) | copy-start | bytes 786436
  4.6 0.7 copy-start.4
  5.3 0.7 copy-start.5
  6.0 0.7 copy-start.6
  6.7 0.7 copy-start.7

commit v2 on v1

v2 whole, which is shorter than its diff:
```python
import functools

import jax
import jax.numpy as jnp
from jax import lax
from jax.experimental import pallas as pl
from jax.experimental.pallas import tpu as pltpu
from jax.sharding import PartitionSpec as P

BLOCK = 64
LONGEST = 2048
EPS = 1e-06
FAR = -1e30
MESH = pl.DeviceIdType.MESH
f32 = jnp.float32
bf16 = jnp.bfloat16


def mm(a, b):
    return lax.dot_general(a, b, (((1,), (0,)), ((), ())), preferred_element_type=f32)


def mm_t(a, b):
    return lax.dot_general(a, b, (((1,), (1,)), ((), ())), preferred_element_type=f32)


def split(x):
    hi = x.astype(bf16)
    return hi, (x - hi.astype(f32)).astype(bf16)


def iota(shape, dim):
    return lax.broadcasted_iota(jnp.int32, shape, dim)


def split3(x):
    first = x.astype(bf16)
    rest = x - first.astype(f32)
    second = rest.astype(bf16)
    return first, second, (rest - second.astype(f32)).astype(bf16)


def seg_of(pos, ends):
    total = jnp.zeros_like(pos)
    for end in ends:
        total = total + (pos >= end).astype(jnp.int32)
    return total


def vectors(gate, beta):
    heads, tokens = gate.shape
    n = 2 * BLOCK
    blocks = tokens // BLOCK
    left = []
    for b in range(blocks):
        at = slice(b * BLOCK, (b + 1) * BLOCK)
        part = gate[:, at]
        left.append(jnp.concatenate([part, jnp.zeros_like(part)], axis=1))
        left.append(jnp.concatenate([beta[0][:, at], beta[1][:, at]], axis=1))
    left = jnp.concatenate(left, axis=0)
    count = left.shape[0]
    k, r = iota((n, n), 0), iota((n, n), 1)
    upto = ((k < BLOCK) & (k <= r // 2)).astype(f32)
    place = (r == 2 * (k % BLOCK) + k // BLOCK).astype(f32)
    token = ((k < BLOCK) & (k <= r)).astype(f32)
    table = jnp.concatenate([upto, place, token], axis=1).astype(bf16)
    got = mm(jnp.concatenate(split3(left), axis=0), table)
    got = got[:count] + got[count : 2 * count] + got[2 * count :]
    both = 2 * heads
    first = iota((both, n), 0) < heads
    rows, toks = [], []
    for b in range(blocks):
        mine = got[b * both : (b + 1) * both]
        rows.append(jnp.where(first, mine[:, :n], mine[:, n : 2 * n]))
        toks.append(mine[:, 2 * n :])
    return rows, toks


def block_masks(offset, ends, block):
    n = 2 * BLOCK
    start = offset + block * BLOCK
    before = sum((start - 1 >= e).astype(jnp.int32) for e in ends)
    before = jnp.where(start == 0, -1, before)
    last = sum((start + BLOCK - 1 >= e).astype(jnp.int32) for e in ends)
    seg_row = seg_of(start + iota((1, n), 1) // 2, ends)
    seg_col = seg_of(start + iota((n, 1), 0) // 2, ends)
    seg_tok = seg_of(start + iota((BLOCK, 1), 0), ends)
    i, j = iota((n, n), 0), iota((n, n), 1)
    pair = jnp.where((i >= j) & (seg_col == seg_row), 0.0, FAR)
    ti, tj = iota((BLOCK, n), 0), iota((BLOCK, n), 1)
    read = jnp.where((ti >= tj // 2) & (seg_tok == seg_row), 0.0, FAR)
    carry_row = jnp.where(seg_row == before, 0.0, FAR)
    carry_tok = jnp.where(seg_tok == before, 0.0, FAR)
    end_row = jnp.where(seg_row == last, 0.0, FAR)
    return pair, read, carry_row, carry_tok, end_row


def level_mask(n, level):
    i, j = iota((n, n), 0), iota((n, n), 1)
    return ((i > j) & (lax.shift_right_logical(i ^ j, level) == 1)).astype(f32).astype(bf16)


def levels_of(n):
    return n.bit_length() - 1


def as_cols(rows):
    cols = jnp.transpose(jnp.concatenate(rows, axis=0))
    return [cols[:, u : u + 1] for u in range(len(rows))]


def state_maps(units, masks, eye, levels):
    n = eye.shape[0]
    width = units[0][0].shape[1]
    eye16 = eye.astype(bf16)
    grams = [mm_t(k, k) for k, *_ in units]
    norms = [
        lax.rsqrt(jnp.sum(gram * eye, axis=0, keepdims=True) + EPS) for gram in grams
    ]
    beta_cols = as_cols([norm * unit[4] for norm, unit in zip(norms, units)])
    end_cols = as_cols(
        [
            jnp.exp((unit[2][:, n - 1 :] - unit[2]) + mask[4]) * norm
            for norm, unit, mask in zip(norms, units, masks)
        ]
    )
    lowers = []
    for gram, norm, beta_col, (k, v, c_row, c_col, b_row), mask in zip(
        grams, norms, beta_cols, units, masks
    ):
        ratio = jnp.exp((c_col - c_row) + mask[0])
        lower = (beta_col * ratio) * (norm * gram)
        lowers.append(split(lower - lower * eye))
    xs = [eye16 - low[0] * levels(0) for low in lowers]
    for level in range(1, levels_of(n)):
        mask = levels(level)
        ys = [mm(low[0] * mask, x).astype(bf16) for low, x in zip(lowers, xs)]
        xs = [x - mm(x, y).astype(bf16) for x, y in zip(xs, ys)]
    lefts = [
        mm(jnp.concatenate(low, axis=1), jnp.concatenate([x, x], axis=0))
        for low, x in zip(lowers, xs)
    ]
    rests = [((eye - x.astype(f32)) - left).astype(bf16) for x, left in zip(xs, lefts)]
    invs = [x.astype(f32) + mm(x, rest) for x, rest in zip(xs, rests)]
    writes = []
    for inv, norm, (k, v, c_row, c_col, b_row), mask in zip(invs, norms, units, masks):
        for_value = inv * b_row
        for_key = inv * (b_row * jnp.exp(c_row + mask[2]) * norm)
        wv = mm(jnp.concatenate(split(for_value), axis=1), jnp.concatenate([v, v], axis=0))
        wk = mm(jnp.concatenate(split(for_key), axis=1), jnp.concatenate([k, k], axis=0))
        writes.append(jnp.concatenate([wv, wk], axis=1))
    outs = []
    for write, end, norm, (k, v, c_row, c_col, b_row), mask in zip(
        writes, end_cols, norms, units, masks
    ):
        hi, lo = split(write * end)
        kt = jnp.transpose(k)
        ew = mm(jnp.concatenate([kt, kt], axis=1), jnp.concatenate([hi, lo], axis=0))
        carry_last = jnp.exp(c_row[:, n - 1 :] + mask[2][:, n - 1 :])
        outs.append((carry_last * eye - ew[:, width:], ew[:, :width], write.astype(bf16), norm))
    return outs


def compose(maps):
    width = maps[0][0].shape[1]
    totals = [jnp.concatenate(maps[0], axis=1)]
    for map_b, add_b in maps[1:]:
        hi, lo = split(totals[-1])
        m_hi, m_lo = split(map_b)
        total = mm(jnp.concatenate([m_hi, m_lo], axis=1), jnp.concatenate([hi, hi], axis=0))
        total = total + mm(m_hi, lo)
        totals.append(jnp.concatenate([total[:, :width], total[:, width:] + add_b], axis=1))
    return totals


def block_reads(q, k, write, norm, c_row, ct_col, mask, before):
    width = q.shape[1]
    qf = q.astype(f32)
    nq = lax.rsqrt(jnp.sum(qf * qf, axis=1, keepdims=True) + EPS) * width**-0.5
    weights = (jnp.exp((ct_col - c_row) + mask[1]) * nq) * (norm * mm_t(q, k))
    got = mm(weights.astype(bf16), write)
    reads = (jnp.exp(ct_col + mask[3]) * nq) * qf - got[:, width:]
    if before is None:
        return reads.astype(bf16), got[:, :width]
    wide = mm(reads.astype(bf16), before)
    return wide[:, :width].astype(bf16), got[:, :width] + wide[:, width:]


def kernel(
    n_seq,
    n_head,
    rounds,
    q_hbm,
    k_hbm,
    v_hbm,
    beta_hbm,
    gate_hbm,
    len_hbm,
    gain_hbm,
    w_hbm,
    out_ref,
    q_s,
    k_s,
    v_s,
    w_s,
    beta_s,
    gate_s,
    len_s,
    gain_s,
    row_s,
    col_s,
    tok_s,
    pair_s,
    read_s,
    crow_s,
    ctok_s,
    erow_s,
    eye_s,
    lev_s,
    write_s,
    norm_s,
    before_s,
    map_s,
    add_s,
    g_s,
    o_s,
    send_s,
    recv_s,
    flat_s,
    part_s,
    relay_s,
    sum_s,
    got_s,
    in_sem,
    small_sem,
    w_sem,
    ring_send,
    ring_recv,
    relay_send,
    relay_recv,
    x_send,
    x_recv,
):
    z = lax.axis_index("seq")
    x = lax.axis_index("head")
    heads, subs, width = k_s.shape
    tokens = q_s.shape[1]
    blocks = tokens // BLOCK
    n = 2 * BLOCK
    right, left = lax.rem(x + 1, n_head), lax.rem(x + n_head - 1, n_head)
    has_before, has_after = z > 0, z < n_seq - 1

    smalls = [
        pltpu.make_async_copy(src, dst, small_sem.at[i])
        for i, (src, dst) in enumerate(
            ((len_hbm, len_s), (gate_hbm, gate_s), (beta_hbm, beta_s), (gain_hbm, gain_s))
        )
    ]
    for copy in smalls:
        copy.start()
    k_rows = k_hbm.reshape(subs, heads * width)
    v_rows = v_hbm.reshape(subs, heads * width)

    def loads(h):
        lanes = pl.ds(pl.multiple_of(h * width, width), width)
        return (
            pltpu.make_async_copy(k_rows.at[:, lanes], k_s.at[h], in_sem.at[0, h]),
            pltpu.make_async_copy(v_rows.at[:, lanes], v_s.at[h], in_sem.at[1, h]),
            pltpu.make_async_copy(q_hbm.at[:, lanes], q_s.at[h], in_sem.at[2, h]),
        )

    for h in range(heads):
        for copy in loads(h)[:2]:
            copy.start()
    for h in range(heads):
        loads(h)[2].start()
    w_copy = pltpu.make_async_copy(w_hbm, w_s, w_sem)
    w_copy.start()

    barrier = pltpu.get_barrier_semaphore()
    for side in (right, left):
        pl.semaphore_signal(barrier, inc=1, device_id={"head": side}, device_id_type=MESH)

    @pl.when(has_before)
    def _():
        pl.semaphore_signal(barrier, inc=1, device_id={"seq": z - 1}, device_id_type=MESH)

    eye_s[...] = (iota((n, n), 0) == iota((n, n), 1)).astype(f32)
    for level in range(levels_of(n)):
        lev_s[level] = level_mask(n, level)
    for copy in smalls:
        copy.wait()
    offset = z * tokens
    ends, run = [], 0
    for i in range(len_s.shape[0]):
        run = run + len_s[i]
        ends.append(run)
    rows, toks = vectors(gate_s[...], [beta_s[j] for j in range(2)])
    for b in range(blocks):
        cols = jnp.transpose(rows[b])
        t_cols = jnp.transpose(toks[b])
        for h in range(heads):
            row_s[h, b] = rows[b][h : h + 1]
            row_s[heads + h, b] = rows[b][heads + h : heads + h + 1]
            col_s[h, b] = cols[:, h : h + 1]
            tok_s[h, b] = t_cols[:BLOCK, h : h + 1]
        pair_s[b], read_s[b], crow_s[b], ctok_s[b], erow_s[b] = block_masks(offset, ends, b)

    @pl.when(jnp.logical_not(has_before))
    def _():
        recv_s[...] = jnp.zeros_like(recv_s)

    def hop(r, h):
        return pltpu.make_async_remote_copy(
            src_ref=send_s.at[r, h],
            dst_ref=recv_s.at[r, h],
            send_sem=ring_send.at[r, h],
            recv_sem=ring_recv.at[r, h],
            device_id={"seq": jnp.minimum(z + 1, n_seq - 1)},
            device_id_type=MESH,
        )

    def leave(r, h, state):
        send_s[r, h] = state.astype(bf16)

        @pl.when(has_after)
        def _():
            hop(r, h).start()

    def arrive(r, h):
        @pl.when(has_before)
        def _():
            hop(r, h).wait_recv()

        return recv_s[r, h]

    def masks_of(b):
        return pair_s[b], read_s[b], crow_s[b], ctok_s[b], erow_s[b]

    def two_heads(pair, carry):
        hs = [2 * pair, 2 * pair + 1]
        units, masks = [], []
        for h in hs:
            for copy in loads(h)[:2]:
                copy.wait()
        for h in hs:
            for b in range(blocks):
                at = pl.ds(b * n, n)
                units.append(
                    (
                        k_s[h, at, :],
                        v_s[h, at, :],
                        row_s[h, b],
                        col_s[h, b],
                        row_s[heads + h, b],
                    )
                )
                masks.append(masks_of(b))
        outs = state_maps(units, masks, eye_s[...], lambda l: lev_s[l])

        totals = [
            compose([m[:2] for m in outs[i * blocks : (i + 1) * blocks]]) for i in range(len(hs))
        ]

        @pl.when(pair == 0)
        def _():
            pl.semaphore_wait(barrier, 2 + has_after.astype(jnp.int32))

        for h, total in zip(hs, totals):
            leave(0, h, total[-1][:, width:])
        for i, h in enumerate(hs):
            for b in range(blocks):
                write_s[h, b] = outs[i * blocks + b][2]
                norm_s[h, b] = outs[i * blocks + b][3]
            for b in range(1, blocks):
                before_s[h, b - 1] = totals[i][b - 1].astype(bf16)
            map_s[h] = jnp.concatenate(split(totals[i][-1][:, :width]), axis=1)
            add_s[h] = totals[i][-1][:, width:]
        return carry

    lax.fori_loop(0, heads // 2, two_heads, 0)

    def step(r):
        for h in range(heads):
            got = arrive(r - 1, h)
            leave(r, h, add_s[h] + mm(map_s[h], jnp.concatenate([got, got], axis=0)))

    def reads_and_step(h, carry):
        loads(h)[2].wait()
        for b in range(blocks):
            at = pl.ds(b * BLOCK, BLOCK)
            g_s[h, at, :], o_s[h, at, :] = block_reads(
                q_s[h, at, :],
                k_s[h, pl.ds(b * n, n), :],
                write_s[h, b],
                norm_s[h, b],
                row_s[h, b],
                tok_s[h, b],
                masks_of(b),
                before_s[h, b - 1] if b else None,
            )

        step(h + 1)
        return carry

    def just_step(r, carry):
        step(r)
        return carry

    lax.fori_loop(0, heads, reads_and_step, 0)
    lax.fori_loop(heads + 1, rounds, just_step, 0)

    for h in range(heads):
        got = arrive(rounds - 1, h)
        out = o_s[h] + mm(g_s[h], got)
        mean = jnp.sum(out * out, axis=1, keepdims=True) * (1.0 / width)
        flat_s[:, h * width : (h + 1) * width] = (
            out * lax.rsqrt(mean + EPS) * gain_s[...]
        ).astype(bf16)

    chunks, _, chunk = part_s.shape
    share = out_ref.shape[0]
    lower = chunks // 2
    far = lax.rem(x + 2, n_head)

    def rows_for(dest):
        return pl.ds(pl.multiple_of(dest * share, share), share)

    def relay(c):
        return pltpu.make_async_remote_copy(
            src_ref=part_s.at[c, rows_for(far), :],
            dst_ref=relay_s.at[c],
            send_sem=relay_send.at[c],
            recv_sem=relay_recv.at[c],
            device_id={"head": right if c < lower else left},
            device_id_type=MESH,
        )

    def direct(c):
        to = left if c < lower else right
        return pltpu.make_async_remote_copy(
            src_ref=part_s.at[c, rows_for(to), :],
            dst_ref=got_s.at[0, c],
            send_sem=x_send.at[0, c],
            recv_sem=x_recv.at[0, c],
            device_id={"head": to},
            device_id_type=MESH,
        )

    def summed(c):
        to = right if c < lower else left
        return pltpu.make_async_remote_copy(
            src_ref=sum_s.at[c],
            dst_ref=got_s.at[1, c],
            send_sem=x_send.at[1, c],
            recv_sem=x_recv.at[1, c],
            device_id={"head": to},
            device_id_type=MESH,
        )

    order = [c for pair in zip(range(lower), range(lower, chunks)) for c in pair]
    w_copy.wait()
    flat = flat_s[...]
    for c in order:
        part_s[c] = mm(flat, w_s[:, c * chunk : (c + 1) * chunk]).astype(bf16)
        relay(c).start()
    for c in order:
        direct(c).start()
    for c in order:
        relay(c).wait_recv()
        to = right if c < lower else left
        sum_s[c] = (part_s[c, rows_for(to), :].astype(f32) + relay_s[c].astype(f32)).astype(bf16)
        summed(c).start()
    for c in order:
        direct(c).wait_recv()
        total = part_s[c, rows_for(x), :].astype(f32) + got_s[0, c].astype(f32)
        summed(c).wait_recv()
        out_ref[:, c * chunk : (c + 1) * chunk] = (total + got_s[1, c].astype(f32)).astype(bf16)

    @pl.when(has_after)
    def _():
        def drain(r, carry):
            for h in range(heads):
                hop(r, h).wait_send()
            return carry

        lax.fori_loop(0, rounds, drain, 0)

    for c in order:
        relay(c).wait_send()
        direct(c).wait_send()
        summed(c).wait_send()


def solution(mesh):
    n_seq, n_head = mesh.shape["seq"], mesh.shape["head"]

    def body(queries, keys, values, beta, gate, lengths, gain, weight):
        tokens, lanes = queries.shape[1:]
        refl, heads = beta.shape[2:]
        width = lanes // heads
        subs = tokens * refl
        blocks = tokens // BLOCK
        n = refl * BLOCK
        model = weight.shape[1]
        share = tokens // n_head
        rounds = min(n_seq - 1, -(-LONGEST // tokens))
        chunks = 4
        chunk = model // chunks
        hbm = pl.BlockSpec(memory_space=pltpu.HBM)
        vmem = pl.BlockSpec(memory_space=pltpu.VMEM)
        dma = pltpu.SemaphoreType.DMA
        out = pl.pallas_call(
            functools.partial(kernel, n_seq, n_head, rounds),
            out_shape=jax.ShapeDtypeStruct((share, model), bf16),
            in_specs=[hbm] * 8,
            out_specs=vmem,
            scratch_shapes=[
                pltpu.VMEM((heads, tokens, width), bf16),
                pltpu.VMEM((heads, subs, width), bf16),
                pltpu.VMEM((heads, subs, width), bf16),
                pltpu.VMEM((lanes, model), bf16),
                pltpu.VMEM((refl, heads, tokens), f32),
                pltpu.VMEM((heads, tokens), f32),
                pltpu.SMEM((lengths.shape[1],), jnp.int32),
                pltpu.VMEM((1, width), f32),
                pltpu.VMEM((2 * heads, blocks, 1, n), f32),
                pltpu.VMEM((heads, blocks, n, 1), f32),
                pltpu.VMEM((heads, blocks, BLOCK, 1), f32),
                pltpu.VMEM((blocks, n, n), f32),
                pltpu.VMEM((blocks, BLOCK, n), f32),
                pltpu.VMEM((blocks, 1, n), f32),
                pltpu.VMEM((blocks, BLOCK, 1), f32),
                pltpu.VMEM((blocks, 1, n), f32),
                pltpu.VMEM((n, n), f32),
                pltpu.VMEM((levels_of(n), n, n), bf16),
                pltpu.VMEM((heads, blocks, n, 2 * width), bf16),
                pltpu.VMEM((heads, blocks, 1, n), f32),
                pltpu.VMEM((heads, blocks - 1, width, 2 * width), bf16),
                pltpu.VMEM((heads, width, 2 * width), bf16),
                pltpu.VMEM((heads, width, width), f32),
                pltpu.VMEM((heads, tokens, width), bf16),
                pltpu.VMEM((heads, tokens, width), f32),
                pltpu.VMEM((rounds, heads, width, width), bf16),
                pltpu.VMEM((rounds, heads, width, width), bf16),
                pltpu.VMEM((tokens, lanes), bf16),
                pltpu.VMEM((chunks, tokens, chunk), bf16),
                pltpu.VMEM((chunks, share, chunk), bf16),
                pltpu.VMEM((chunks, share, chunk), bf16),
                pltpu.VMEM((2, chunks, share, chunk), bf16),
                dma((3, heads)),
                dma((4,)),
                dma,
                dma((rounds, heads)),
                dma((rounds, heads)),
                dma((chunks,)),
                dma((chunks,)),
                dma((2, chunks)),
                dma((2, chunks)),
            ],
            compiler_params=pltpu.CompilerParams(
                collective_id=0, has_side_effects=True, vmem_limit_bytes=67043328
            ),
        )(
            queries[0],
            keys[0],
            values[0],
            jnp.transpose(beta[0], (1, 2, 0)),
            jnp.transpose(gate[0], (1, 0)),
            lengths[0],
            gain[None, :],
            weight,
        )
        return out[None]

    packs = ("parts", "rep")
    in_specs = (
        P(packs, "seq", "head"),
        P(packs, "seq", None, "head"),
        P(packs, "seq", None, "head"),
        P(packs, "seq", None, "head"),
        P(packs, "seq", "head"),
        P(packs, None),
        P(),
        P("head", None),
    )
    out_specs = P(packs, ("seq", "head"), None)
    return jax.shard_map(body, mesh=mesh, in_specs=in_specs, out_specs=out_specs, check_vma=False)
```

time: 84.9 us -> 53.9 us (0.63)
  the two profiles are of different devices: /device:TPU:40 before, /device:TPU:288 now
where the time goes in v2:
time: 53.9 us; the launch traced here: 53.8 us
  Pallas kernels  52.1 us (97%)
  local copies, waits for them, and re-layouts  1.67 us (3%)
    pallas_call x1, Pallas kernels, body(): pl.pallas_call(functools.partial(kernel, n_seq, n_head, rounds), out_shap...  52.1 us
    unnamed x1, local copies, waits for them, and re-layouts  1.67 us

profile of v2, /device:TPU:288, one launch (start us, length us, event | category | flops | bytes accessed | tf_op | source)
XLA Modules:
  0.0 53.8 jit_solution(15709288951781027413)
XLA Ops:
  0.0 52.1 %shard_map.82 = bf16[64,2048]{1,0:T(8,128)(2,1)} custom-call(bf16[256,512]{1,0:T(8,128)(2,1)} %bitcast.15, bf16[256,2,512]{2,1,0:T(2,128)(2,1)} %bitcast.13, bf16[256,2,512]{2,1,0:T(2,128)(2,1)} %bitcast.14, f32[2,4,256]{2,1,0:T(4,128)} %bitcast.16, f32[4,256]{1,0:T(4,128)} %bitcast.17, s32[6]{0:T(128)} %bitcast.18, f32[1,128]{1,0:T(1,128)} %bitcast.19, ...), custom_call_target="tpu_custom_call" | custom-call | tf_op jit(solution)/shard_map/pallas_call | solution.py:513
  52.1 1.7 %copy.10 = bf16[1,64,2048]{2,1,0:T(8,128)(2,1)} copy(bf16[1,64,2048]{2,1,0:T(8,128)(2,1)} %bitcast.12) | data formatting | bytes 524288

commit v3 on v2

--- a/solution.py
+++ b/solution.py
@@ -249,6 +249,8 @@
     n = 2 * BLOCK
     right, left = lax.rem(x + 1, n_head), lax.rem(x + n_head - 1, n_head)
     has_before, has_after = z > 0, z < n_seq - 1
+    rounds_in = jnp.minimum(rounds, z)
+    rounds_out = jnp.where(has_after, jnp.minimum(rounds, z + 1), 0)
 
     smalls = [
         pltpu.make_async_copy(src, dst, small_sem.at[i])
@@ -308,7 +310,7 @@
 
     @pl.when(jnp.logical_not(has_before))
     def _():
-        recv_s[...] = jnp.zeros_like(recv_s)
+        recv_s[0] = jnp.zeros_like(recv_s[0])
 
     def hop(r, h):
         return pltpu.make_async_remote_copy(
@@ -319,20 +321,6 @@
             device_id={"seq": jnp.minimum(z + 1, n_seq - 1)},
             device_id_type=MESH,
         )
-
-    def leave(r, h, state):
-        send_s[r, h] = state.astype(bf16)
-
-        @pl.when(has_after)
-        def _():
-            hop(r, h).start()
-
-    def arrive(r, h):
-        @pl.when(has_before)
-        def _():
-            hop(r, h).wait_recv()
-
-        return recv_s[r, h]
 
     def masks_of(b):
         return pair_s[b], read_s[b], crow_s[b], ctok_s[b], erow_s[b]
@@ -367,7 +355,13 @@
             pl.semaphore_wait(barrier, 2 + has_after.astype(jnp.int32))
 
         for h, total in zip(hs, totals):
-            leave(0, h, total[-1][:, width:])
+            send_s[0, h] = total[-1][:, width:].astype(bf16)
+
+        @pl.when(has_after)
+        def _():
+            for h in hs:
+                hop(0, h).start()
+
         for i, h in enumerate(hs):
             for b in range(blocks):
                 write_s[h, b] = outs[i * blocks + b][2]
@@ -382,8 +376,11 @@
 
     def step(r):
         for h in range(heads):
-            got = arrive(r - 1, h)
-            leave(r, h, add_s[h] + mm(map_s[h], jnp.concatenate([got, got], axis=0)))
+            hop(r - 1, h).wait_recv()
+            got = recv_s[r - 1, h]
+            state = add_s[h] + mm(map_s[h], jnp.concatenate([got, got], axis=0))
+            send_s[r, h] = state.astype(bf16)
+            hop(r, h).start()
 
     def reads_and_step(h, carry):
         loads(h)[2].wait()
@@ -400,7 +397,10 @@
                 before_s[h, b - 1] if b else None,
             )
 
-        step(h + 1)
+        @pl.when(h + 1 < rounds_out)
+        def _():
+            step(h + 1)
+
         return carry
 
     def just_step(r, carry):
@@ -408,10 +408,25 @@
         return carry
 
     lax.fori_loop(0, heads, reads_and_step, 0)
-    lax.fori_loop(heads + 1, rounds, just_step, 0)
-
+    lax.fori_loop(heads + 1, rounds_out, just_step, 0)
+
+    @pl.when(jnp.logical_not(has_after))
+    def _():
+        def skip(r, carry):
+            for h in range(heads):
+                hop(r, h).wait_recv()
+            return carry
+
+        lax.fori_loop(0, rounds_in - 1, skip, 0)
+
+    last = jnp.maximum(rounds_in - 1, 0)
     for h in range(heads):
-        got = arrive(rounds - 1, h)
+
+        @pl.when(rounds_in >= jnp.maximum(rounds_out, 1))
+        def _():
+            hop(last, h).wait_recv()
+
+        got = recv_s[last, h]
         out = o_s[h] + mm(g_s[h], got)
         mean = jnp.sum(out * out, axis=1, keepdims=True) * (1.0 / width)
         flat_s[:, h * width : (h + 1) * width] = (
@@ -477,15 +492,12 @@
         summed(c).wait_recv()
         out_ref[:, c * chunk : (c + 1) * chunk] = (total + got_s[1, c].astype(f32)).astype(bf16)
 
-    @pl.when(has_after)
-    def _():
-        def drain(r, carry):
-            for h in range(heads):
-                hop(r, h).wait_send()
-            return carry
-
-        lax.fori_loop(0, rounds, drain, 0)
-
+    def drain(r, carry):
+        for h in range(heads):
+            hop(r, h).wait_send()
+        return carry
+
+    lax.fori_loop(0, rounds_out, drain, 0)
     for c in order:
         relay(c).wait_send()
         direct(c).wait_send()
@@ -559,9 +571,12 @@
                 dma((2, chunks)),
             ],
             compiler_params=pltpu.CompilerParams(
-                collective_id=0, has_side_effects=True, vmem_limit_bytes=67043328
+                collective_id=0, has_side_effects=True, vmem_limit_bytes=40 * 1024 * 1024
             ),
         )(
+            *[
+                pltpu.with_memory_space_constraint(a, pltpu.HBM)
+                for a in (
             queries[0],
             keys[0],
             values[0],
@@ -570,6 +585,8 @@
             lengths[0],
             gain[None, :],
             weight,
+                )
+            ]
         )
         return out[None]
 

time: 53.9 us -> 50.3 us (0.933)
  the two profiles are of different devices: /device:TPU:288 before, /device:TPU:1056 now
where the time goes in v3:
time: 50.3 us; the launch traced here: 50.2 us
  Pallas kernels  49.5 us (98%)
  local copies, waits for them, and re-layouts  0.71 us (1%)
    pallas_call x1, Pallas kernels, body(): pl.pallas_call(functools.partial(kernel, n_seq, n_head, rounds), out_shap...  49.5 us

profile of v3, /device:TPU:1056, one launch (start us, length us, event | category | flops | bytes accessed | tf_op | source)
XLA Modules:
  0.0 50.2 jit_solution(901316399504255241)
XLA Ops:
  0.0 49.5 %shard_map.82 = bf16[64,2048]{1,0:T(8,128)(2,1)S(1)} custom-call(bf16[256,512]{1,0:T(8,128)(2,1)} %bitcast.15, bf16[256,2,512]{2,1,0:T(2,128)(2,1)} %bitcast.13, bf16[256,2,512]{2,1,0:T(2,128)(2,1)} %bitcast.14, f32[2,4,256]{2,1,0:T(4,128)} %bitcast.16, f32[4,256]{1,0:T(4,128)} %bitcast.17, s32[6]{0:T(128)} %bitcast.18, f32[1,128]{1,0:T(1,128)} %bitcast.19, ...), custom_call_target="tpu_custom_call" | custom-call | tf_op jit(solution)/shard_map/pallas_call | solution.py:525
  49.5 0.7 %copy.10 = bf16[1,64,2048]{2,1,0:T(8,128)(2,1)} copy(bf16[1,64,2048]{2,1,0:T(8,128)(2,1)S(1)} %bitcast.12) | data formatting | bytes 524288

commit v4 on v3

--- a/solution.py
+++ b/solution.py
@@ -249,8 +249,14 @@
     n = 2 * BLOCK
     right, left = lax.rem(x + 1, n_head), lax.rem(x + n_head - 1, n_head)
     has_before, has_after = z > 0, z < n_seq - 1
-    rounds_in = jnp.minimum(rounds, z)
-    rounds_out = jnp.where(has_after, jnp.minimum(rounds, z + 1), 0)
+    odd = lax.rem(z, 2)
+    first = 1 - odd
+    ages = jnp.where(has_after, (jnp.minimum(rounds, z - 1) - first + 2) // 2, 0)
+    ages = jnp.where(z > 0, ages, 0)
+    lead = has_after & (z < rounds)
+    last = jnp.where(z <= rounds, z - 1, jnp.where(odd == 1, rounds - 1, rounds))
+    last = jnp.maximum(last, 0)
+    starts = has_after & ((odd == 1) | (z == 0))
 
     smalls = [
         pltpu.make_async_copy(src, dst, small_sem.at[i])
@@ -357,7 +363,7 @@
         for h, total in zip(hs, totals):
             send_s[0, h] = total[-1][:, width:].astype(bf16)
 
-        @pl.when(has_after)
+        @pl.when(starts)
         def _():
             for h in hs:
                 hop(0, h).start()
@@ -381,6 +387,11 @@
             state = add_s[h] + mm(map_s[h], jnp.concatenate([got, got], axis=0))
             send_s[r, h] = state.astype(bf16)
             hop(r, h).start()
+
+    def next_age(i):
+        @pl.when((i < ages) & (first + 2 * i > 0))
+        def _():
+            step(first + 2 * i)
 
     def reads_and_step(h, carry):
         loads(h)[2].wait()
@@ -397,32 +408,33 @@
                 before_s[h, b - 1] if b else None,
             )
 
-        @pl.when(h + 1 < rounds_out)
-        def _():
-            step(h + 1)
-
+        next_age(h)
         return carry
 
-    def just_step(r, carry):
-        step(r)
+    def just_step(i, carry):
+        next_age(i)
         return carry
 
     lax.fori_loop(0, heads, reads_and_step, 0)
-    lax.fori_loop(heads + 1, rounds_out, just_step, 0)
+    lax.fori_loop(heads, ages, just_step, 0)
+
+    @pl.when(lead & (z > 0))
+    def _():
+        step(z)
 
     @pl.when(jnp.logical_not(has_after))
     def _():
-        def skip(r, carry):
+        def skip(i, carry):
             for h in range(heads):
-                hop(r, h).wait_recv()
+                hop(1 + 2 * i, h).wait_recv()
             return carry
 
-        lax.fori_loop(0, rounds_in - 1, skip, 0)
-
-    last = jnp.maximum(rounds_in - 1, 0)
+        lax.fori_loop(0, (rounds - 1) // 2, skip, 0)
+
+    waits = jnp.logical_not(has_after) | ((odd == 0) & (z >= rounds))
     for h in range(heads):
 
-        @pl.when(rounds_in >= jnp.maximum(rounds_out, 1))
+        @pl.when(waits)
         def _():
             hop(last, h).wait_recv()
 
@@ -492,12 +504,18 @@
         summed(c).wait_recv()
         out_ref[:, c * chunk : (c + 1) * chunk] = (total + got_s[1, c].astype(f32)).astype(bf16)
 
-    def drain(r, carry):
+    def drain(i, carry):
         for h in range(heads):
-            hop(r, h).wait_send()
+            hop(first + 2 * i, h).wait_send()
         return carry
 
-    lax.fori_loop(0, rounds_out, drain, 0)
+    lax.fori_loop(0, ages, drain, 0)
+
+    @pl.when(lead)
+    def _():
+        for h in range(heads):
+            hop(z, h).wait_send()
+
     for c in order:
         relay(c).wait_send()
         direct(c).wait_send()
@@ -553,8 +571,8 @@
                 pltpu.VMEM((heads, width, width), f32),
                 pltpu.VMEM((heads, tokens, width), bf16),
                 pltpu.VMEM((heads, tokens, width), f32),
-                pltpu.VMEM((rounds, heads, width, width), bf16),
-                pltpu.VMEM((rounds, heads, width, width), bf16),
+                pltpu.VMEM((rounds + 1, heads, width, width), bf16),
+                pltpu.VMEM((rounds + 1, heads, width, width), bf16),
                 pltpu.VMEM((tokens, lanes), bf16),
                 pltpu.VMEM((chunks, tokens, chunk), bf16),
                 pltpu.VMEM((chunks, share, chunk), bf16),
@@ -563,8 +581,8 @@
                 dma((3, heads)),
                 dma((4,)),
                 dma,
-                dma((rounds, heads)),
-                dma((rounds, heads)),
+                dma((rounds + 1, heads)),
+                dma((rounds + 1, heads)),
                 dma((chunks,)),
                 dma((chunks,)),
                 dma((2, chunks)),

time: 50.3 us -> 50.3 us (level)
  no operation moved by 1% of the time
where the time goes in v4:
time: 50.3 us; the launch traced here: 50.2 us
  Pallas kernels  49.5 us (98%)
  local copies, waits for them, and re-layouts  0.71 us (1%)
    pallas_call x1, Pallas kernels, body(): pl.pallas_call(functools.partial(kernel, n_seq, n_head, rounds), out_shap...  49.5 us

profile of v4, /device:TPU:1056, one launch (start us, length us, event | category | flops | bytes accessed | tf_op | source)
XLA Modules:
  0.0 50.2 jit_solution(7798276495068566874)
XLA Ops:
  0.0 49.5 %shard_map.82 = bf16[64,2048]{1,0:T(8,128)(2,1)S(1)} custom-call(bf16[256,512]{1,0:T(8,128)(2,1)} %bitcast.15, bf16[256,2,512]{2,1,0:T(2,128)(2,1)} %bitcast.13, bf16[256,2,512]{2,1,0:T(2,128)(2,1)} %bitcast.14, f32[2,4,256]{2,1,0:T(4,128)} %bitcast.16, f32[4,256]{1,0:T(4,128)} %bitcast.17, s32[6]{0:T(128)} %bitcast.18, f32[1,128]{1,0:T(1,128)} %bitcast.19, ...), custom_call_target="tpu_custom_call" | custom-call | tf_op jit(solution)/shard_map/pallas_call | solution.py:543
  49.5 0.7 %copy.10 = bf16[1,64,2048]{2,1,0:T(8,128)(2,1)} copy(bf16[1,64,2048]{2,1,0:T(8,128)(2,1)S(1)} %bitcast.12) | data formatting | bytes 524288

commit v5 on v3

--- a/solution.py
+++ b/solution.py
@@ -226,6 +226,9 @@
     o_s,
     send_s,
     recv_s,
+    up_s,
+    own_s,
+    enter_s,
     flat_s,
     part_s,
     relay_s,
@@ -234,6 +237,8 @@
     in_sem,
     small_sem,
     w_sem,
+    near_send,
+    near_recv,
     ring_send,
     ring_recv,
     relay_send,
@@ -249,8 +254,13 @@
     n = 2 * BLOCK
     right, left = lax.rem(x + 1, n_head), lax.rem(x + n_head - 1, n_head)
     has_before, has_after = z > 0, z < n_seq - 1
-    rounds_in = jnp.minimum(rounds, z)
-    rounds_out = jnp.where(has_after, jnp.minimum(rounds, z + 1), 0)
+    odd = lax.rem(z, 2) == 1
+    even = jnp.logical_not(odd)
+    pair_at = z // 2
+    reach = rounds // 2
+    passes = jnp.minimum(reach, pair_at + 1)
+    last = jnp.maximum(jnp.minimum(reach, pair_at) - 1, 0)
+    relays = odd & has_after
 
     smalls = [
         pltpu.make_async_copy(src, dst, small_sem.at[i])
@@ -286,6 +296,10 @@
     @pl.when(has_before)
     def _():
         pl.semaphore_signal(barrier, inc=1, device_id={"seq": z - 1}, device_id_type=MESH)
+
+    @pl.when(odd & (z > 1))
+    def _():
+        pl.semaphore_signal(barrier, inc=1, device_id={"seq": z - 2}, device_id_type=MESH)
 
     eye_s[...] = (iota((n, n), 0) == iota((n, n), 1)).astype(f32)
     for level in range(levels_of(n)):
@@ -310,17 +324,32 @@
 
     @pl.when(jnp.logical_not(has_before))
     def _():
-        recv_s[0] = jnp.zeros_like(recv_s[0])
-
-    def hop(r, h):
+        enter_s[...] = jnp.zeros_like(enter_s)
+
+    def to_next(what, src, dst, sem, h, step):
         return pltpu.make_async_remote_copy(
-            src_ref=send_s.at[r, h],
-            dst_ref=recv_s.at[r, h],
-            send_sem=ring_send.at[r, h],
-            recv_sem=ring_recv.at[r, h],
-            device_id={"seq": jnp.minimum(z + 1, n_seq - 1)},
+            src_ref=src,
+            dst_ref=dst,
+            send_sem=sem[0].at[what, h],
+            recv_sem=sem[1].at[what, h],
+            device_id={"seq": jnp.minimum(z + step, n_seq - 1)},
             device_id_type=MESH,
         )
+
+    near = (near_send, near_recv)
+    ring = (ring_send, ring_recv)
+
+    def up_add(h):
+        return to_next(0, send_s.at[0, h], up_s.at[0, h], near, h, 1)
+
+    def up_map(h):
+        return to_next(1, own_s.at[h], up_s.at[1, h], near, h, 1)
+
+    def down(h):
+        return to_next(2, send_s.at[passes - 1, h], enter_s.at[h], near, h, 1)
+
+    def hop(r, h):
+        return to_next(r, send_s.at[r, h], recv_s.at[r, h], ring, h, 2)
 
     def masks_of(b):
         return pair_s[b], read_s[b], crow_s[b], ctok_s[b], erow_s[b]
@@ -352,15 +381,17 @@
 
         @pl.when(pair == 0)
         def _():
-            pl.semaphore_wait(barrier, 2 + has_after.astype(jnp.int32))
+            pl.semaphore_wait(
+                barrier, 2 + has_after.astype(jnp.int32) + relays.astype(jnp.int32)
+            )
 
         for h, total in zip(hs, totals):
             send_s[0, h] = total[-1][:, width:].astype(bf16)
 
-        @pl.when(has_after)
+        @pl.when(even)
         def _():
             for h in hs:
-                hop(0, h).start()
+                up_add(h).start()
 
         for i, h in enumerate(hs):
             for b in range(blocks):
@@ -368,19 +399,52 @@
                 norm_s[h, b] = outs[i * blocks + b][3]
             for b in range(1, blocks):
                 before_s[h, b - 1] = totals[i][b - 1].astype(bf16)
-            map_s[h] = jnp.concatenate(split(totals[i][-1][:, :width]), axis=1)
+            hi, lo = split(totals[i][-1][:, :width])
+            own_s[h] = hi
+            map_s[h] = jnp.concatenate([hi, lo], axis=1)
             add_s[h] = totals[i][-1][:, width:]
+
+        @pl.when(even)
+        def _():
+            for h in hs:
+                up_map(h).start()
+
         return carry
 
     lax.fori_loop(0, heads // 2, two_heads, 0)
+
+    def twice(a):
+        return jnp.concatenate([a, a], axis=0)
+
+    def join():
+        for h in range(heads):
+            up_add(h).wait_recv()
+            add = add_s[h] + mm(map_s[h], twice(up_s[0, h]))
+            send_s[0, h] = add.astype(bf16)
+            add_s[h] = add
+
+            @pl.when(has_after)
+            def _():
+                hop(0, h).start()
+
+            @pl.when(pair_at == 0)
+            def _():
+                down(h).start()
+
+        for h in range(heads):
+            up_map(h).wait_recv()
+            map_s[h] = jnp.concatenate(split(mm(map_s[h], twice(up_s[1, h]))), axis=1)
 
     def step(r):
         for h in range(heads):
             hop(r - 1, h).wait_recv()
-            got = recv_s[r - 1, h]
-            state = add_s[h] + mm(map_s[h], jnp.concatenate([got, got], axis=0))
+            state = add_s[h] + mm(map_s[h], twice(recv_s[r - 1, h]))
             send_s[r, h] = state.astype(bf16)
             hop(r, h).start()
+
+            @pl.when(r == passes - 1)
+            def _():
+                down(h).start()
 
     def reads_and_step(h, carry):
         loads(h)[2].wait()
@@ -397,9 +461,13 @@
                 before_s[h, b - 1] if b else None,
             )
 
-        @pl.when(h + 1 < rounds_out)
-        def _():
-            step(h + 1)
+        @pl.when(odd & (h == 1))
+        def _():
+            join()
+
+        @pl.when(relays & (h > 1) & (h - 1 < passes))
+        def _():
+            step(h - 1)
 
         return carry
 
@@ -408,7 +476,7 @@
         return carry
 
     lax.fori_loop(0, heads, reads_and_step, 0)
-    lax.fori_loop(heads + 1, rounds_out, just_step, 0)
+    lax.fori_loop(heads - 1, jnp.where(relays, passes, 0), just_step, 0)
 
     @pl.when(jnp.logical_not(has_after))
     def _():
@@ -417,17 +485,28 @@
                 hop(r, h).wait_recv()
             return carry
 
-        lax.fori_loop(0, rounds_in - 1, skip, 0)
-
-    last = jnp.maximum(rounds_in - 1, 0)
+        lax.fori_loop(0, last, skip, 0)
+
     for h in range(heads):
 
-        @pl.when(rounds_in >= jnp.maximum(rounds_out, 1))
+        @pl.when(even & has_before)
+        def _():
+            down(h).wait_recv()
+
+        @pl.when(odd & (pair_at == 0))
+        def _():
+            enter_s[h] = up_s[0, h]
+
+        @pl.when(odd & (pair_at >= reach))
         def _():
             hop(last, h).wait_recv()
 
-        got = recv_s[last, h]
-        out = o_s[h] + mm(g_s[h], got)
+        @pl.when(odd & (pair_at > 0))
+        def _():
+            state = up_s[0, h].astype(f32) + mm(up_s[1, h], recv_s[last, h])
+            enter_s[h] = state.astype(bf16)
+
+        out = o_s[h] + mm(g_s[h], enter_s[h])
         mean = jnp.sum(out * out, axis=1, keepdims=True) * (1.0 / width)
         flat_s[:, h * width : (h + 1) * width] = (
             out * lax.rsqrt(mean + EPS) * gain_s[...]
@@ -497,7 +576,19 @@
             hop(r, h).wait_send()
         return carry
 
-    lax.fori_loop(0, rounds_out, drain, 0)
+    lax.fori_loop(0, jnp.where(relays, passes, 0), drain, 0)
+
+    @pl.when(relays)
+    def _():
+        for h in range(heads):
+            down(h).wait_send()
+
+    @pl.when(even)
+    def _():
+        for h in range(heads):
+            up_add(h).wait_send()
+            up_map(h).wait_send()
+
     for c in order:
         relay(c).wait_send()
         direct(c).wait_send()
@@ -516,7 +607,7 @@
         n = refl * BLOCK
         model = weight.shape[1]
         share = tokens // n_head
-        rounds = min(n_seq - 1, -(-LONGEST // tokens))
+        rounds = -(-LONGEST // tokens)
         chunks = 4
         chunk = model // chunks
         hbm = pl.BlockSpec(memory_space=pltpu.HBM)
@@ -553,8 +644,11 @@
                 pltpu.VMEM((heads, width, width), f32),
                 pltpu.VMEM((heads, tokens, width), bf16),
                 pltpu.VMEM((heads, tokens, width), f32),
-                pltpu.VMEM((rounds, heads, width, width), bf16),
-                pltpu.VMEM((rounds, heads, width, width), bf16),
+                pltpu.VMEM((rounds // 2, heads, width, width), bf16),
+                pltpu.VMEM((rounds // 2, heads, width, width), bf16),
+                pltpu.VMEM((2, heads, width, width), bf16),
+                pltpu.VMEM((heads, width, width), bf16),
+                pltpu.VMEM((heads, width, width), bf16),
                 pltpu.VMEM((tokens, lanes), bf16),
                 pltpu.VMEM((chunks, tokens, chunk), bf16),
                 pltpu.VMEM((chunks, share, chunk), bf16),
@@ -563,8 +657,10 @@
                 dma((3, heads)),
                 dma((4,)),
                 dma,
-                dma((rounds, heads)),
-                dma((rounds, heads)),
+                dma((3, heads)),
+                dma((3, heads)),
+                dma((rounds // 2, heads)),
+                dma((rounds // 2, heads)),
                 dma((chunks,)),
                 dma((chunks,)),
                 dma((2, chunks)),

time: 50.3 us -> 48.4 us (0.962)
  the two profiles are of different devices: /device:TPU:1056 before, /device:TPU:1320 now
where the time goes in v5:
time: 48.4 us; the launch traced here: 48.3 us
  Pallas kernels  47.6 us (98%)
  local copies, waits for them, and re-layouts  0.71 us (1%)
    pallas_call x1, Pallas kernels, body(): pl.pallas_call(functools.partial(kernel, n_seq, n_head, rounds), out_shap...  47.6 us

profile of v5, /device:TPU:1320, one launch (start us, length us, event | category | flops | bytes accessed | tf_op | source)
XLA Modules:
  0.0 48.3 jit_solution(1691155995883020362)
XLA Ops:
  0.0 47.6 %shard_map.82 = bf16[64,2048]{1,0:T(8,128)(2,1)S(1)} custom-call(bf16[256,512]{1,0:T(8,128)(2,1)} %bitcast.15, bf16[256,2,512]{2,1,0:T(2,128)(2,1)} %bitcast.13, bf16[256,2,512]{2,1,0:T(2,128)(2,1)} %bitcast.14, f32[2,4,256]{2,1,0:T(4,128)} %bitcast.16, f32[4,256]{1,0:T(4,128)} %bitcast.17, s32[6]{0:T(128)} %bitcast.18, f32[1,128]{1,0:T(1,128)} %bitcast.19, ...), custom_call_target="tpu_custom_call" | custom-call | tf_op jit(solution)/shard_map/pallas_call | solution.py:616
  47.6 0.7 %copy.10 = bf16[1,64,2048]{2,1,0:T(8,128)(2,1)} copy(bf16[1,64,2048]{2,1,0:T(8,128)(2,1)S(1)} %bitcast.12) | data formatting | bytes 524288

commit v6 on v5

--- a/solution.py
+++ b/solution.py
@@ -258,9 +258,17 @@
     even = jnp.logical_not(odd)
     pair_at = z // 2
     reach = rounds // 2
-    passes = jnp.minimum(reach, pair_at + 1)
-    last = jnp.maximum(jnp.minimum(reach, pair_at) - 1, 0)
     relays = odd & has_after
+    odd_pair = lax.rem(pair_at, 2)
+
+    def incoming(pair):
+        late = jnp.where(lax.rem(pair, 2) == 1, reach - 1, reach)
+        return jnp.where(pair <= reach, pair - 1, late)
+
+    last = jnp.maximum(incoming(pair_at), 0)
+    down_at = incoming(pair_at + 1)
+    starts = relays & ((odd_pair == 1) | (pair_at == 0))
+    lead = relays & (pair_at < reach)
 
     smalls = [
         pltpu.make_async_copy(src, dst, small_sem.at[i])
@@ -346,7 +354,7 @@
         return to_next(1, own_s.at[h], up_s.at[1, h], near, h, 1)
 
     def down(h):
-        return to_next(2, send_s.at[passes - 1, h], enter_s.at[h], near, h, 1)
+        return to_next(2, send_s.at[down_at, h], enter_s.at[h], near, h, 1)
 
     def hop(r, h):
         return to_next(r, send_s.at[r, h], recv_s.at[r, h], ring, h, 2)
@@ -423,7 +431,7 @@
             send_s[0, h] = add.astype(bf16)
             add_s[h] = add
 
-            @pl.when(has_after)
+            @pl.when(starts)
             def _():
                 hop(0, h).start()
 
@@ -442,7 +450,7 @@
             send_s[r, h] = state.astype(bf16)
             hop(r, h).start()
 
-            @pl.when(r == passes - 1)
+            @pl.when(r == down_at)
             def _():
                 down(h).start()
 
@@ -465,28 +473,30 @@
         def _():
             join()
 
-        @pl.when(relays & (h > 1) & (h - 1 < passes))
-        def _():
-            step(h - 1)
+        age = 1 - odd_pair + 2 * (h - 2 + odd_pair)
+
+        @pl.when(relays & (h > 1) & (age <= jnp.minimum(reach, pair_at - 1)))
+        def _():
+            step(age)
 
         return carry
 
-    def just_step(r, carry):
-        step(r)
-        return carry
-
     lax.fori_loop(0, heads, reads_and_step, 0)
-    lax.fori_loop(heads - 1, jnp.where(relays, passes, 0), just_step, 0)
+
+    @pl.when(lead & (pair_at > 0))
+    def _():
+        step(pair_at)
 
     @pl.when(jnp.logical_not(has_after))
     def _():
-        def skip(r, carry):
+        def skip(i, carry):
             for h in range(heads):
-                hop(r, h).wait_recv()
+                hop(1 + 2 * i, h).wait_recv()
             return carry
 
-        lax.fori_loop(0, last, skip, 0)
-
+        lax.fori_loop(0, (reach - 1) // 2, skip, 0)
+
+    waits = odd & (jnp.logical_not(has_after) | ((odd_pair == 0) & (pair_at >= reach)))
     for h in range(heads):
 
         @pl.when(even & has_before)
@@ -497,7 +507,7 @@
         def _():
             enter_s[h] = up_s[0, h]
 
-        @pl.when(odd & (pair_at >= reach))
+        @pl.when(waits)
         def _():
             hop(last, h).wait_recv()
 
@@ -571,12 +581,14 @@
         summed(c).wait_recv()
         out_ref[:, c * chunk : (c + 1) * chunk] = (total + got_s[1, c].astype(f32)).astype(bf16)
 
-    def drain(r, carry):
-        for h in range(heads):
-            hop(r, h).wait_send()
-        return carry
-
-    lax.fori_loop(0, jnp.where(relays, passes, 0), drain, 0)
+    for r in range(reach + 1):
+        sent = lax.rem(r + odd_pair, 2) == 1
+        sent = sent & (r < pair_at)
+
+        @pl.when(relays & (sent | (lead & (pair_at == r))))
+        def _():
+            for h in range(heads):
+                hop(r, h).wait_send()
 
     @pl.when(relays)
     def _():
@@ -644,8 +656,8 @@
                 pltpu.VMEM((heads, width, width), f32),
                 pltpu.VMEM((heads, tokens, width), bf16),
                 pltpu.VMEM((heads, tokens, width), f32),
-                pltpu.VMEM((rounds // 2, heads, width, width), bf16),
-                pltpu.VMEM((rounds // 2, heads, width, width), bf16),
+                pltpu.VMEM((rounds // 2 + 1, heads, width, width), bf16),
+                pltpu.VMEM((rounds // 2 + 1, heads, width, width), bf16),
                 pltpu.VMEM((2, heads, width, width), bf16),
                 pltpu.VMEM((heads, width, width), bf16),
                 pltpu.VMEM((heads, width, width), bf16),
@@ -659,8 +671,8 @@
                 dma,
                 dma((3, heads)),
                 dma((3, heads)),
-                dma((rounds // 2, heads)),
-                dma((rounds // 2, heads)),
+                dma((rounds // 2 + 1, heads)),
+                dma((rounds // 2 + 1, heads)),
                 dma((chunks,)),
                 dma((chunks,)),
                 dma((2, chunks)),

time: 48.4 us -> 44.6 us (0.921)
  the two profiles are of different devices: /device:TPU:1320 before, /device:TPU:160 now
where the time goes in v6:
time: 44.6 us; the launch traced here: 44.5 us
  Pallas kernels  43.8 us (98%)
  local copies, waits for them, and re-layouts  0.71 us (2%)
    pallas_call x1, Pallas kernels, body(): pl.pallas_call(functools.partial(kernel, n_seq, n_head, rounds), out_shap...  43.8 us

profile of v6, /device:TPU:160, one launch (start us, length us, event | category | flops | bytes accessed | tf_op | source)
XLA Modules:
  0.0 44.5 jit_solution(15810211799095072288)
XLA Ops:
  0.0 43.8 %shard_map.82 = bf16[64,2048]{1,0:T(8,128)(2,1)S(1)} custom-call(bf16[256,512]{1,0:T(8,128)(2,1)} %bitcast.15, bf16[256,2,512]{2,1,0:T(2,128)(2,1)} %bitcast.13, bf16[256,2,512]{2,1,0:T(2,128)(2,1)} %bitcast.14, f32[2,4,256]{2,1,0:T(4,128)} %bitcast.16, f32[4,256]{1,0:T(4,128)} %bitcast.17, s32[6]{0:T(128)} %bitcast.18, f32[1,128]{1,0:T(1,128)} %bitcast.19, ...), custom_call_target="tpu_custom_call" | custom-call | tf_op jit(solution)/shard_map/pallas_call | solution.py:628
  43.8 0.7 %copy.10 = bf16[1,64,2048]{2,1,0:T(8,128)(2,1)} copy(bf16[1,64,2048]{2,1,0:T(8,128)(2,1)S(1)} %bitcast.12) | data formatting | bytes 524288

commit v7 on v6

--- a/solution.py
+++ b/solution.py
@@ -362,64 +362,41 @@
     def masks_of(b):
         return pair_s[b], read_s[b], crow_s[b], ctok_s[b], erow_s[b]
 
-    def two_heads(pair, carry):
-        hs = [2 * pair, 2 * pair + 1]
-        units, masks = [], []
-        for h in hs:
-            for copy in loads(h)[:2]:
-                copy.wait()
-        for h in hs:
-            for b in range(blocks):
-                at = pl.ds(b * n, n)
-                units.append(
-                    (
-                        k_s[h, at, :],
-                        v_s[h, at, :],
-                        row_s[h, b],
-                        col_s[h, b],
-                        row_s[heads + h, b],
-                    )
-                )
-                masks.append(masks_of(b))
-        outs = state_maps(units, masks, eye_s[...], lambda l: lev_s[l])
-
-        totals = [
-            compose([m[:2] for m in outs[i * blocks : (i + 1) * blocks]]) for i in range(len(hs))
-        ]
-
-        @pl.when(pair == 0)
-        def _():
-            pl.semaphore_wait(
-                barrier, 2 + has_after.astype(jnp.int32) + relays.astype(jnp.int32)
+    units, masks = [], []
+    for h in range(heads):
+        for copy in loads(h)[:2]:
+            copy.wait()
+    for h in range(heads):
+        for b in range(blocks):
+            at = pl.ds(b * n, n)
+            units.append(
+                (k_s[h, at, :], v_s[h, at, :], row_s[h, b], col_s[h, b], row_s[heads + h, b])
             )
-
-        for h, total in zip(hs, totals):
-            send_s[0, h] = total[-1][:, width:].astype(bf16)
-
-        @pl.when(even)
-        def _():
-            for h in hs:
-                up_add(h).start()
-
-        for i, h in enumerate(hs):
-            for b in range(blocks):
-                write_s[h, b] = outs[i * blocks + b][2]
-                norm_s[h, b] = outs[i * blocks + b][3]
-            for b in range(1, blocks):
-                before_s[h, b - 1] = totals[i][b - 1].astype(bf16)
-            hi, lo = split(totals[i][-1][:, :width])
-            own_s[h] = hi
-            map_s[h] = jnp.concatenate([hi, lo], axis=1)
-            add_s[h] = totals[i][-1][:, width:]
-
-        @pl.when(even)
-        def _():
-            for h in hs:
-                up_map(h).start()
-
-        return carry
-
-    lax.fori_loop(0, heads // 2, two_heads, 0)
+            masks.append(masks_of(b))
+    outs = state_maps(units, masks, eye_s[...], lambda l: lev_s[l])
+    totals = [compose([m[:2] for m in outs[h * blocks : (h + 1) * blocks]]) for h in range(heads)]
+    for h in range(heads):
+        send_s[0, h] = totals[h][-1][:, width:].astype(bf16)
+        hi, lo = split(totals[h][-1][:, :width])
+        own_s[h] = hi
+        map_s[h] = jnp.concatenate([hi, lo], axis=1)
+
+    pl.semaphore_wait(barrier, 2 + has_after.astype(jnp.int32) + relays.astype(jnp.int32))
+
+    @pl.when(even)
+    def _():
+        for h in range(heads):
+            up_add(h).start()
+        for h in range(heads):
+            up_map(h).start()
+
+    for h in range(heads):
+        add_s[h] = totals[h][-1][:, width:]
+        for b in range(blocks):
+            write_s[h, b] = outs[h * blocks + b][2]
+            norm_s[h, b] = outs[h * blocks + b][3]
+        for b in range(1, blocks):
+            before_s[h, b - 1] = totals[h][b - 1].astype(bf16)
 
     def twice(a):
         return jnp.concatenate([a, a], axis=0)
@@ -454,34 +431,41 @@
             def _():
                 down(h).start()
 
-    def reads_and_step(h, carry):
-        loads(h)[2].wait()
-        for b in range(blocks):
-            at = pl.ds(b * BLOCK, BLOCK)
-            g_s[h, at, :], o_s[h, at, :] = block_reads(
-                q_s[h, at, :],
-                k_s[h, pl.ds(b * n, n), :],
-                write_s[h, b],
-                norm_s[h, b],
-                row_s[h, b],
-                tok_s[h, b],
-                masks_of(b),
-                before_s[h, b - 1] if b else None,
-            )
-
-        @pl.when(odd & (h == 1))
+    def reads_and_join(i, carry):
+        for h in (2 * i, 2 * i + 1):
+            loads(h)[2].wait()
+        for h in (2 * i, 2 * i + 1):
+            for b in range(blocks):
+                at = pl.ds(b * BLOCK, BLOCK)
+                g_s[h, at, :], o_s[h, at, :] = block_reads(
+                    q_s[h, at, :],
+                    k_s[h, pl.ds(b * n, n), :],
+                    write_s[h, b],
+                    norm_s[h, b],
+                    row_s[h, b],
+                    tok_s[h, b],
+                    masks_of(b),
+                    before_s[h, b - 1] if b else None,
+                )
+
+        @pl.when(odd & (i == (pair_at == 0).astype(jnp.int32)))
         def _():
             join()
 
-        age = 1 - odd_pair + 2 * (h - 2 + odd_pair)
-
-        @pl.when(relays & (h > 1) & (age <= jnp.minimum(reach, pair_at - 1)))
+        return carry
+
+    lax.fori_loop(0, heads // 2, reads_and_join, 0)
+
+    def next_age(i, carry):
+        age = 1 - odd_pair + 2 * (i + odd_pair)
+
+        @pl.when(relays & (age <= jnp.minimum(reach, pair_at - 1)))
         def _():
             step(age)
 
         return carry
 
-    lax.fori_loop(0, heads, reads_and_step, 0)
+    lax.fori_loop(0, reach // 2, next_age, 0)
 
     @pl.when(lead & (pair_at > 0))
     def _():

time: 44.6 us -> 44.8 us (level)
  the two profiles are of different devices: /device:TPU:160 before, /device:TPU:1576 now
where the time goes in v7:
time: 44.8 us; the launch traced here: 44.7 us
  Pallas kernels  43.9 us (98%)
  local copies, waits for them, and re-layouts  0.71 us (2%)
    pallas_call x1, Pallas kernels, body(): pl.pallas_call(functools.partial(kernel, n_seq, n_head, rounds), out_shap...  43.9 us

profile of v7, /device:TPU:1576, one launch (start us, length us, event | category | flops | bytes accessed | tf_op | source)
XLA Modules:
  0.0 44.7 jit_solution(17231761393201693030)
XLA Ops:
  0.0 43.9 %shard_map.82 = bf16[64,2048]{1,0:T(8,128)(2,1)S(1)} custom-call(bf16[256,512]{1,0:T(8,128)(2,1)} %bitcast.15, bf16[256,2,512]{2,1,0:T(2,128)(2,1)} %bitcast.13, bf16[256,2,512]{2,1,0:T(2,128)(2,1)} %bitcast.14, f32[2,4,256]{2,1,0:T(4,128)} %bitcast.16, f32[4,256]{1,0:T(4,128)} %bitcast.17, s32[6]{0:T(128)} %bitcast.18, f32[1,128]{1,0:T(1,128)} %bitcast.19, ...), custom_call_target="tpu_custom_call" | custom-call | tf_op jit(solution)/shard_map/pallas_call | solution.py:612
  44.0 0.7 %copy.10 = bf16[1,64,2048]{2,1,0:T(8,128)(2,1)} copy(bf16[1,64,2048]{2,1,0:T(8,128)(2,1)S(1)} %bitcast.12) | data formatting | bytes 524288

commit v8 on v7

--- a/solution.py
+++ b/solution.py
@@ -259,16 +259,9 @@
     pair_at = z // 2
     reach = rounds // 2
     relays = odd & has_after
-    odd_pair = lax.rem(pair_at, 2)
-
-    def incoming(pair):
-        late = jnp.where(lax.rem(pair, 2) == 1, reach - 1, reach)
-        return jnp.where(pair <= reach, pair - 1, late)
-
-    last = jnp.maximum(incoming(pair_at), 0)
-    down_at = incoming(pair_at + 1)
-    starts = relays & ((odd_pair == 1) | (pair_at == 0))
-    lead = relays & (pair_at < reach)
+    last = (pair_at > reach).astype(jnp.int32)
+    down_at = (pair_at + 1 > reach).astype(jnp.int32)
+    sends = (relays & (pair_at < reach), relays & (pair_at > 0))
 
     smalls = [
         pltpu.make_async_copy(src, dst, small_sem.at[i])
@@ -405,12 +398,12 @@
         for h in range(heads):
             up_add(h).wait_recv()
             add = add_s[h] + mm(map_s[h], twice(up_s[0, h]))
-            send_s[0, h] = add.astype(bf16)
             add_s[h] = add
 
-            @pl.when(starts)
+            @pl.when(relays & (pair_at < 2))
             def _():
-                hop(0, h).start()
+                send_s[pair_at, h] = add.astype(bf16)
+                hop(pair_at, h).start()
 
             @pl.when(pair_at == 0)
             def _():
@@ -422,8 +415,8 @@
 
     def step(r):
         for h in range(heads):
-            hop(r - 1, h).wait_recv()
-            state = add_s[h] + mm(map_s[h], twice(recv_s[r - 1, h]))
+            hop(r, h).wait_recv()
+            state = add_s[h] + mm(map_s[h], twice(recv_s[r, h]))
             send_s[r, h] = state.astype(bf16)
             hop(r, h).start()
 
@@ -456,31 +449,17 @@
 
     lax.fori_loop(0, heads // 2, reads_and_join, 0)
 
-    def next_age(i, carry):
-        age = 1 - odd_pair + 2 * (i + odd_pair)
-
-        @pl.when(relays & (age <= jnp.minimum(reach, pair_at - 1)))
+    def next_chain(i, carry):
+        r = 1 - i
+
+        @pl.when((sends[1] & (r == 1) & (pair_at > 1)) | (sends[0] & (r == 0) & (pair_at > 0)))
         def _():
-            step(age)
+            step(r)
 
         return carry
 
-    lax.fori_loop(0, reach // 2, next_age, 0)
-
-    @pl.when(lead & (pair_at > 0))
-    def _():
-        step(pair_at)
-
-    @pl.when(jnp.logical_not(has_after))
-    def _():
-        def skip(i, carry):
-            for h in range(heads):
-                hop(1 + 2 * i, h).wait_recv()
-            return carry
-
-        lax.fori_loop(0, (reach - 1) // 2, skip, 0)
-
-    waits = odd & (jnp.logical_not(has_after) | ((odd_pair == 0) & (pair_at >= reach)))
+    lax.fori_loop(0, 2, next_chain, 0)
+    waits = odd & (jnp.logical_not(has_after) | (pair_at == reach))
     for h in range(heads):
 
         @pl.when(even & has_before)
@@ -565,11 +544,9 @@
         summed(c).wait_recv()
         out_ref[:, c * chunk : (c + 1) * chunk] = (total + got_s[1, c].astype(f32)).astype(bf16)
 
-    for r in range(reach + 1):
-        sent = lax.rem(r + odd_pair, 2) == 1
-        sent = sent & (r < pair_at)
-
-        @pl.when(relays & (sent | (lead & (pair_at == r))))
+    for r in range(2):
+
+        @pl.when(sends[r])
         def _():
             for h in range(heads):
                 hop(r, h).wait_send()
@@ -604,6 +581,7 @@
         model = weight.shape[1]
         share = tokens // n_head
         rounds = -(-LONGEST // tokens)
+        assert rounds % 2 == 0 and n_seq % 2 == 0 and n_seq // 2 > rounds // 2 + 1
         chunks = 4
         chunk = model // chunks
         hbm = pl.BlockSpec(memory_space=pltpu.HBM)
@@ -640,8 +618,8 @@
                 pltpu.VMEM((heads, width, width), f32),
                 pltpu.VMEM((heads, tokens, width), bf16),
                 pltpu.VMEM((heads, tokens, width), f32),
-                pltpu.VMEM((rounds // 2 + 1, heads, width, width), bf16),
-                pltpu.VMEM((rounds // 2 + 1, heads, width, width), bf16),
+                pltpu.VMEM((2, heads, width, width), bf16),
+                pltpu.VMEM((2, heads, width, width), bf16),
                 pltpu.VMEM((2, heads, width, width), bf16),
                 pltpu.VMEM((heads, width, width), bf16),
                 pltpu.VMEM((heads, width, width), bf16),
@@ -655,8 +633,8 @@
                 dma,
                 dma((3, heads)),
                 dma((3, heads)),
-                dma((rounds // 2 + 1, heads)),
-                dma((rounds // 2 + 1, heads)),
+                dma((2, heads)),
+                dma((2, heads)),
                 dma((chunks,)),
                 dma((chunks,)),
                 dma((2, chunks)),

time: 44.8 us -> 41.8 us (0.933)
  the two profiles are of different devices: /device:TPU:1576 before, /device:TPU:1056 now
where the time goes in v8:
time: 41.8 us; the launch traced here: 41.7 us
  Pallas kernels  41 us (98%)
  local copies, waits for them, and re-layouts  0.71 us (2%)
    pallas_call x1, Pallas kernels, body(): pl.pallas_call(functools.partial(kernel, n_seq, n_head, rounds), out_shap...  41 us

profile of v8, /device:TPU:1056, one launch (start us, length us, event | category | flops | bytes accessed | tf_op | source)
XLA Modules:
  0.0 41.7 jit_solution(9185009911610086958)
XLA Ops:
  0.0 41.0 %shard_map.82 = bf16[64,2048]{1,0:T(8,128)(2,1)S(1)} custom-call(bf16[256,512]{1,0:T(8,128)(2,1)} %bitcast.15, bf16[256,2,512]{2,1,0:T(2,128)(2,1)} %bitcast.13, bf16[256,2,512]{2,1,0:T(2,128)(2,1)} %bitcast.14, f32[2,4,256]{2,1,0:T(4,128)} %bitcast.16, f32[4,256]{1,0:T(4,128)} %bitcast.17, s32[6]{0:T(128)} %bitcast.18, f32[1,128]{1,0:T(1,128)} %bitcast.19, ...), custom_call_target="tpu_custom_call" | custom-call | tf_op jit(solution)/shard_map/pallas_call | solution.py:590
  41.0 0.7 %copy.10 = bf16[1,64,2048]{2,1,0:T(8,128)(2,1)} copy(bf16[1,64,2048]{2,1,0:T(8,128)(2,1)S(1)} %bitcast.12) | data formatting | bytes 524288

commit v9 on v8

--- a/solution.py
+++ b/solution.py
@@ -161,16 +161,24 @@
     return outs
 
 
+def after(later, earlier):
+    width = later.shape[0]
+    hi, lo = split(earlier)
+    m_hi, m_lo = split(later[:, :width])
+    total = mm(jnp.concatenate([m_hi, m_lo], axis=1), jnp.concatenate([hi, hi], axis=0))
+    total = total + mm(m_hi, lo)
+    return jnp.concatenate([total[:, :width], total[:, width:] + later[:, width:]], axis=1)
+
+
 def compose(maps):
-    width = maps[0][0].shape[1]
-    totals = [jnp.concatenate(maps[0], axis=1)]
-    for map_b, add_b in maps[1:]:
-        hi, lo = split(totals[-1])
-        m_hi, m_lo = split(map_b)
-        total = mm(jnp.concatenate([m_hi, m_lo], axis=1), jnp.concatenate([hi, hi], axis=0))
-        total = total + mm(m_hi, lo)
-        totals.append(jnp.concatenate([total[:, :width], total[:, width:] + add_b], axis=1))
-    return totals
+    first, second, third, fourth = (jnp.concatenate(m, axis=1) for m in maps)
+    width = third.shape[0]
+    early = after(second, first)
+    whole = after(after(fourth, third), early)
+    early16 = early.astype(bf16)
+    three = mm(third[:, :width].astype(bf16), early16)
+    three = jnp.concatenate([three[:, :width], three[:, width:] + third[:, width:]], axis=1)
+    return first.astype(bf16), early16, three.astype(bf16), whole
 
 
 def block_reads(q, k, write, norm, c_row, ct_col, mask, before):
@@ -389,7 +397,7 @@
             write_s[h, b] = outs[h * blocks + b][2]
             norm_s[h, b] = outs[h * blocks + b][3]
         for b in range(1, blocks):
-            before_s[h, b - 1] = totals[h][b - 1].astype(bf16)
+            before_s[h, b - 1] = totals[h][b - 1]
 
     def twice(a):
         return jnp.concatenate([a, a], axis=0)
@@ -409,9 +417,11 @@
             def _():
                 down(h).start()
 
-        for h in range(heads):
-            up_map(h).wait_recv()
-            map_s[h] = jnp.concatenate(split(mm(map_s[h], twice(up_s[1, h]))), axis=1)
+        @pl.when(pair_at > 0)
+        def _():
+            for h in range(heads):
+                up_map(h).wait_recv()
+                map_s[h] = jnp.concatenate(split(mm(map_s[h], twice(up_s[1, h]))), axis=1)
 
     def step(r):
         for h in range(heads):
@@ -562,6 +572,11 @@
             up_add(h).wait_send()
             up_map(h).wait_send()
 
+    @pl.when(odd & (pair_at == 0))
+    def _():
+        for h in range(heads):
+            up_map(h).wait_recv()
+
     for c in order:
         relay(c).wait_send()
         direct(c).wait_send()
@@ -581,8 +596,8 @@
         model = weight.shape[1]
         share = tokens // n_head
         rounds = -(-LONGEST // tokens)
-        assert rounds % 2 == 0 and n_seq % 2 == 0 and n_seq // 2 > rounds // 2 + 1
-        chunks = 4
+        assert blocks == 4 and rounds % 2 == 0 and n_seq % 2 == 0 and n_seq // 2 > rounds // 2 + 1
+        chunks = 8
         chunk = model // chunks
         hbm = pl.BlockSpec(memory_space=pltpu.HBM)
         vmem = pl.BlockSpec(memory_space=pltpu.VMEM)

time: 41.8 us -> 42.3 us (1.012)
  Pallas kernels: 41 us -> 41.5 us
    pallas_call x1, Pallas kernels: 41 us -> 41.5 us  [body(): pl.pallas_call(functools.partial(kernel, n_seq, n_head, rounds), out_shap...]
where the time goes in v9:
time: 42.3 us; the launch traced here: 42.2 us
  Pallas kernels  41.5 us (98%)
  local copies, waits for them, and re-layouts  0.71 us (2%)
    pallas_call x1, Pallas kernels, body(): pl.pallas_call(functools.partial(kernel, n_seq, n_head, rounds), out_shap...  41.5 us

profile of v9, /device:TPU:1056, one launch (start us, length us, event | category | flops | bytes accessed | tf_op | source)
XLA Modules:
  0.0 42.2 jit_solution(4932615990847035461)
XLA Ops:
  0.0 41.5 %shard_map.82 = bf16[64,2048]{1,0:T(8,128)(2,1)S(1)} custom-call(bf16[256,512]{1,0:T(8,128)(2,1)} %bitcast.15, bf16[256,2,512]{2,1,0:T(2,128)(2,1)} %bitcast.13, bf16[256,2,512]{2,1,0:T(2,128)(2,1)} %bitcast.14, f32[2,4,256]{2,1,0:T(4,128)} %bitcast.16, f32[4,256]{1,0:T(4,128)} %bitcast.17, s32[6]{0:T(128)} %bitcast.18, f32[1,128]{1,0:T(1,128)} %bitcast.19, ...), custom_call_target="tpu_custom_call" | custom-call | tf_op jit(solution)/shard_map/pallas_call | solution.py:605
  41.5 0.7 %copy.10 = bf16[1,64,2048]{2,1,0:T(8,128)(2,1)} copy(bf16[1,64,2048]{2,1,0:T(8,128)(2,1)S(1)} %bitcast.12) | data formatting | bytes 524288

commit v10 on v9

--- a/solution.py
+++ b/solution.py
@@ -597,7 +597,7 @@
         share = tokens // n_head
         rounds = -(-LONGEST // tokens)
         assert blocks == 4 and rounds % 2 == 0 and n_seq % 2 == 0 and n_seq // 2 > rounds // 2 + 1
-        chunks = 8
+        chunks = 4
         chunk = model // chunks
         hbm = pl.BlockSpec(memory_space=pltpu.HBM)
         vmem = pl.BlockSpec(memory_space=pltpu.VMEM)

time: 42.3 us -> 41.7 us (0.986)
  Pallas kernels: 41.5 us -> 40.9 us
    pallas_call x1, Pallas kernels: 41.5 us -> 40.9 us  [body(): pl.pallas_call(functools.partial(kernel, n_seq, n_head, rounds), out_shap...]
where the time goes in v10:
time: 41.7 us; the launch traced here: 41.6 us
  Pallas kernels  40.9 us (98%)
  local copies, waits for them, and re-layouts  0.71 us (2%)
    pallas_call x1, Pallas kernels, body(): pl.pallas_call(functools.partial(kernel, n_seq, n_head, rounds), out_shap...  40.9 us

profile of v10, /device:TPU:1056, one launch (start us, length us, event | category | flops | bytes accessed | tf_op | source)
XLA Modules:
  0.0 41.6 jit_solution(10238987198805853209)
XLA Ops:
  0.0 40.9 %shard_map.82 = bf16[64,2048]{1,0:T(8,128)(2,1)S(1)} custom-call(bf16[256,512]{1,0:T(8,128)(2,1)} %bitcast.15, bf16[256,2,512]{2,1,0:T(2,128)(2,1)} %bitcast.13, bf16[256,2,512]{2,1,0:T(2,128)(2,1)} %bitcast.14, f32[2,4,256]{2,1,0:T(4,128)} %bitcast.16, f32[4,256]{1,0:T(4,128)} %bitcast.17, s32[6]{0:T(128)} %bitcast.18, f32[1,128]{1,0:T(1,128)} %bitcast.19, ...), custom_call_target="tpu_custom_call" | custom-call | tf_op jit(solution)/shard_map/pallas_call | solution.py:605
  40.9 0.7 %copy.10 = bf16[1,64,2048]{2,1,0:T(8,128)(2,1)} copy(bf16[1,64,2048]{2,1,0:T(8,128)(2,1)S(1)} %bitcast.12) | data formatting | bytes 524288
